TPU v7x, 32 devices: a whole 2x2x4 slice. The times are simulated.
32 devices in a mesh: rep: 1, fsdp: 32 (over z, y, x, core).
Axes of the slice: x: 2, y: 2, z: 4, core: 2. Of those that a mesh axis runs over, the one named last changes fastest.
Arguments:
- accumulated: bfloat16 [1, 2048, 14336], P('rep', 'fsdp'), may hold values from -6 to 6
- q_start: bfloat16 [32, 14336], P(None, 'fsdp'), may hold values from -6 to 6
Outputs:
- residual_buffer: bfloat16 [1, 2048, 14336], P('rep', 'fsdp')
- basis_f32: float32 [2048, 32], P('fsdp')
- q_factor: float32 [32, 14336], P(None, 'fsdp')
All inputs are finite; a program needn't handle non-finite values.
Results may differ from a plain program's by a relative error of at most 0.0039.
Values may be sent and summed in bfloat16 or wider, within the bound.
No kernel may reach another device: no remote copies, remote signals or barrier semaphores. Data moves between devices by JAX's collectives and lax.ppermute only.
A program may use at most 64 MiB of HBM per device.

v0:
```python
import jax
import jax.numpy as jnp
from jax import lax
from jax.sharding import PartitionSpec as P

ITERS = 2


def orthonormal(p_sum):
    partial_gram = jnp.dot(p_sum.T, p_sum, precision=lax.Precision.HIGHEST)
    gram_matrix = lax.psum(partial_gram, "fsdp")
    factor = jnp.linalg.cholesky(gram_matrix)
    return lax.linalg.triangular_solve(factor, p_sum, left_side=False, lower=True, transpose_a=True)


def on_device(accumulated, q_start):
    own_rows = accumulated[0]
    replicas = lax.axis_size("rep")
    shard_cols = q_start.shape[1]
    owner_offset = lax.axis_index("fsdp") * shard_cols
    right_factor = q_start
    for iteration in range(ITERS):
        if iteration == 0:
            term = lax.dot_general(
                own_rows,
                lax.all_gather(q_start, "fsdp", axis=1, tiled=True),
                (((1,), (1,)), ((), ())),
                preferred_element_type=jnp.float32,
            )
            p_local = term
        else:
            p_local = lax.dot_general(
                own_rows, right_factor, (((1,), (1,)), ((), ())), preferred_element_type=jnp.float32
            )
        p_sum = lax.psum(p_local, "rep")
        basis_f32 = orthonormal(p_sum)
        basis_bf16 = basis_f32.astype(jnp.bfloat16)
        q_term = lax.dot_general(
            basis_bf16, own_rows, (((0,), (0,)), ((), ())), preferred_element_type=jnp.float32
        )
        q_whole = lax.psum(q_term, ("rep", "fsdp")) / replicas
        q_owned = lax.dynamic_slice_in_dim(q_whole, owner_offset, shard_cols, 1)
        right_factor = q_whole.astype(jnp.bfloat16)
    approx = lax.dot_general(
        basis_bf16, right_factor, (((1,), (0,)), ((), ())), preferred_element_type=jnp.float32
    )
    residual_buffer = (own_rows.astype(jnp.float32) - approx).astype(jnp.bfloat16)[None]
    return (residual_buffer, basis_f32, q_owned)


def solution(mesh):
    in_specs = (P("rep", "fsdp", None), P(None, "fsdp"))
    out_specs = (P("rep", "fsdp", None), P("fsdp", None), P(None, "fsdp"))
    return jax.shard_map(
        on_device, mesh=mesh, in_specs=in_specs, out_specs=out_specs, check_vma=False
    )
```

profile of v0, /device:TPU:0, one launch (start us, length us, event | category | flops | bytes accessed | tf_op | source)
XLA Modules:
  0.0 356.6 jit_solution(10952083144412553600)
XLA Ops:
  7.2 0.0 all-reduce.3.cloned.1.call-start
  7.2 46.5 %all-gather = bf16[32,448,32]{1,2,0:T(8,128)(2,1)S(1)} all-gather(bf16[1,448,32]{1,2,0:T(8,128)(2,1)} %bitcast.52), channel_id=1, replica_groups=mesh['rep'=1,'fsdp'=32] {'fsdp'}, dimensions={0}, use_global_device_ids=true | all-gather | bytes 946176 | tf_op jit(solution)/shard_map/all_gather | solution.py:26
  53.7 0.0 copy-start
  53.7 0.6 copy.14
  54.2 2.1 reshape.20
  56.4 0.0 copy-done
  56.4 1.8 fusion.8
  58.1 0.2 fusion.24
  58.3 36.9 %psum.26 = f32[32,32]{0,1:T(8,128)S(1)} all-reduce(f32[32,32]{0,1:T(8,128)S(1)} %fusion.24), channel_id=1, replica_groups=mesh['rep'=1,'fsdp'=32] {'fsdp'}, use_global_device_ids=true, to_apply=%region_0.0 | all-reduce | flops 1024 | bytes 8192 | tf_op jit(solution)/shard_map/psum | solution.py:11
  95.2 0.1 copy.16
  95.3 2.9 cholesky.44
  98.3 0.6 compare_reduce_fusion.1
  98.9 0.7 fusion.13
  99.6 2.4 custom-call.6
  102.0 0.2 fusion.10
  102.3 1.6 fusion.6
  103.9 59.3 %all-reduce.4 = bf16[32,14336]{1,0:T(8,128)(2,1)S(1)} all-reduce(f32[32,14336]{1,0:T(8,128)} %fusion.6), channel_id=1, replica_groups=mesh['rep'=1,'fsdp'=32] {'rep','fsdp'}, use_global_device_ids=true, to_apply=%region_3.6 | all-reduce | flops 458752 | bytes 2752512 | tf_op jit(solution)/shard_map/psum | solution.py:41
  163.2 0.6 fusion.4
  163.8 0.2 fusion.25
  164.0 37.5 %psum.36 = f32[32,32]{0,1:T(8,128)S(1)} all-reduce(f32[32,32]{0,1:T(8,128)S(1)} %fusion.25), channel_id=1, replica_groups=mesh['rep'=1,'fsdp'=32] {'fsdp'}, use_global_device_ids=true, to_apply=%region_4.7 | all-reduce | flops 1024 | bytes 8192 | tf_op jit(solution)/shard_map/psum | solution.py:11
  201.4 0.1 copy.18
  201.5 2.9 cholesky.55
  204.5 0.6 compare_reduce_fusion
  205.1 0.7 fusion.14
  205.8 2.4 custom-call.7
  208.2 0.2 convolution_bitcast_fusion
  208.5 0.0 copy-start.1
  208.5 1.6 fusion.2
  210.1 0.0 all-reduce.3.cloned.1.call-update
  210.1 134.6 %all-reduce.3.cloned.1.call-done = f32[32,14336]{1,0:T(8,128)} async-done(((f32[32,14336]{1,0:T(8,128)}), f32[32,14336]{1,0:T(8,128)}) %all-reduce.3.cloned.1.call-update) | async-done | bytes 1835024 | tf_op jit(solution)/shard_map/psum | solution.py:41
  344.7 0.0 copy-done.1
  344.7 3.4 fusion.1
  348.1 1.6 constant_dynamic-slice_fusion
  (4 shorter events, 0.1 us)
Async XLA Ops:
  7.2 337.6 %all-reduce.3.cloned.1.call-start = ((), (), s32[]{:S(2)}) async-start(), calls=%async_computation | async-start | bytes 3670016 | tf_op jit(solution)/shard_map/psum | solution.py:41
  53.7 2.7 copy-start
  208.5 136.3 %copy-start.1 = (f32[64,32]{0,1:T(8,128)}, f32[64,32]{0,1:T(8,128)S(1)}, u32[]{:S(2)}) copy-start(f32[64,32]{0,1:T(8,128)S(1)} %convolution_bitcast_fusion) | copy-start | bytes 24580
Sparse Core Ops, SparseCore 0:
  210.2 134.4 all-reduce.2
where the time goes:
time: 357 us
  blocking collectives  180 us (50%)
  waiting for transfers between devices  135 us (38%)
  between operations  14.1 us (4%)
  other arithmetic  13.4 us (4%)
  matrix products  9.79 us (3%)
  local copies, waits for them, and re-layouts  4.44 us (1%)
    psum x1, waiting for transfers between devices, on_device(): q_whole = lax.psum(q_term, ('rep', 'fsdp')) / replicas  135 us
    psum x2, blocking collectives, orthonormal(): gram_matrix = lax.psum(partial_gram, 'fsdp')  74.4 us
    psum x1, blocking collectives, on_device(): q_whole = lax.psum(q_term, ('rep', 'fsdp')) / replicas  59.3 us
    all_gather x1, blocking collectives, on_device(): lax.all_gather(q_start, 'fsdp', axis=1, tiled=True)  46.5 us
    another operation x6, other arithmetic, orthonormal(): factor = jnp.linalg.cholesky(gram_matrix)  7.19 us
  transfers between devices with their start and end apart: 1, of which 1 were waited for; matrix products, arithmetic and copies ran while one was open for 0% of the time, Pallas kernels for 0%

commit v1 on v0

v1 whole, which is shorter than its diff:
```python
import jax
import jax.numpy as jnp
from jax import lax
from jax.sharding import Mesh, PartitionSpec as P

ITERS = 2
HIGHEST = lax.Precision.HIGHEST
CHIP = ("hi", "lo")
ROWS = ("hi", "lo", "core")
SWAP = ((0, 1), (1, 0))


def transposed_product(left, right):
    return lax.dot_general(left, right, (((0,), (0,)), ((), ())), preferred_element_type=jnp.float32)


def product_transposed(left, right):
    return lax.dot_general(left, right, (((1,), (1,)), ((), ())), preferred_element_type=jnp.float32)


def swap_cores(values):
    return lax.ppermute(values, "core", SWAP)


def spread(values, axis):
    copies = jnp.broadcast_to(values[None], (lax.axis_size(axis),) + values.shape)
    return lax.all_to_all(copies, axis, 0, 0, tiled=True)


def gather_chips(values):
    by_hi = spread(values, "hi")
    return spread(by_hi, "lo").swapaxes(0, 1)


def gather_right(q_half):
    blocks = gather_chips(q_half)
    hi, lo, half, width = blocks.shape
    own = blocks.transpose(2, 0, 1, 3).reshape(half, hi * lo * width)
    return own, swap_cores(own)


def orthonormal_basis(p_rows, p_own):
    own_gram = jnp.dot(p_rows.T, p_rows, precision=HIGHEST)
    gram_matrix = own_gram + swap_cores(own_gram)
    factor = jnp.linalg.cholesky(gram_matrix)
    inverse = lax.linalg.triangular_solve(
        factor, jnp.eye(factor.shape[0], dtype=jnp.float32), left_side=True, lower=True
    )
    basis = lax.dot_general(p_rows, inverse, (((1,), (1,)), ((), ())), precision=HIGHEST)
    basis_own = lax.dot_general(p_own, inverse, (((1,), (1,)), ((), ())), precision=HIGHEST)
    return basis, basis_own


def on_device(accumulated, q_start):
    own_rows = accumulated[0]
    replicas = lax.axis_size("rep")
    chips = lax.axis_size(CHIP)
    core = lax.axis_index("core")
    rows, cols = own_rows.shape
    rank, shard_cols = q_start.shape
    half, width = rank // 2, cols // chips

    blocks = own_rows.reshape(rows, chips, width).transpose(1, 0, 2)
    block = lax.all_to_all(blocks, CHIP, 0, 0, tiled=True).reshape(chips * rows, width)

    kept = lax.dynamic_slice_in_dim(q_start, core * half, half, 0)
    given = lax.dynamic_slice_in_dim(q_start, (1 - core) * half, half, 0)
    taken = swap_cores(given)
    first = jnp.where(core == 0, kept, taken)
    second = jnp.where(core == 0, taken, kept)
    own, other = gather_right(jnp.concatenate([first, second], axis=1))
    p_mine = product_transposed(own_rows, own)
    p_theirs = product_transposed(own_rows, other)
    p_own = jnp.where(
        core == 0,
        jnp.concatenate([p_mine, p_theirs], axis=1),
        jnp.concatenate([p_theirs, p_mine], axis=1),
    )
    for iteration in range(ITERS):
        if iteration > 0:
            term = product_transposed(block, right_factor).reshape(chips, rows, rank)
            p_own = jnp.sum(lax.all_to_all(term, CHIP, 0, 0, tiled=True), axis=0)
        if replicas > 1:
            p_own = lax.psum(p_own, "rep")
        p_rows = spread(p_own, CHIP).reshape(chips * rows, rank)
        basis, basis_own = orthonormal_basis(p_rows, p_own)
        q_term = transposed_product(basis.astype(jnp.bfloat16), block)
        q_chip = q_term + swap_cores(q_term)
        if replicas > 1:
            q_chip = lax.psum(q_chip, "rep")
        q_chip = q_chip / replicas
        right_factor = q_chip.astype(jnp.bfloat16)
    q_owned = lax.dynamic_slice_in_dim(q_chip, core * shard_cols, shard_cols, 1)
    own, other = gather_right(lax.dynamic_slice_in_dim(right_factor, core * half, half, 0))
    basis_bf16 = basis_own.astype(jnp.bfloat16)
    mine = lax.dynamic_slice_in_dim(basis_bf16, core * half, half, 1)
    theirs = lax.dynamic_slice_in_dim(basis_bf16, (1 - core) * half, half, 1)
    approx = lax.dot_general(
        jnp.concatenate([mine, theirs], axis=1),
        jnp.concatenate([own, other], axis=0),
        (((1,), (0,)), ((), ())),
        preferred_element_type=jnp.float32,
    )
    residual_buffer = (own_rows.astype(jnp.float32) - approx).astype(jnp.bfloat16)[None]
    return (residual_buffer, basis_own, q_owned)


def solution(mesh):
    chips = mesh.shape["fsdp"] // 2
    lo = 4
    split = Mesh(
        mesh.devices.reshape(mesh.shape["rep"], chips // lo, lo, 2), ("rep", "hi", "lo", "core")
    )
    in_specs = (P("rep", ROWS, None), P(None, ROWS))
    out_specs = (P("rep", ROWS, None), P(ROWS, None), P(None, ROWS))
    return jax.shard_map(
        on_device, mesh=split, in_specs=in_specs, out_specs=out_specs, check_vma=False
    )
```

time: 357 us -> 155 us (0.43)
  blocking collectives: 180 us -> 67.5 us
  waiting for transfers between devices: 135 us -> 40.2 us
  between operations: 14.1 us -> 0.95 us
  starting transfers between devices: 0.04 us -> 9.23 us
  other arithmetic: 13.4 us -> 17.1 us
  local copies, waits for them, and re-layouts: 4.44 us -> 8.08 us
    psum x1 -> x0, waiting for transfers between devices: 135 us -> none  [on_device(): q_whole = lax.psum(q_term, ('rep', 'fsdp')) / replicas]
    psum x3 -> x0, blocking collectives: 134 us -> none  [the longest x2 74.4 us: orthonormal(): gram_matrix = lax.psum(partial_gram, 'fsdp')]
    all_to_all x0 -> x6, blocking collectives: none -> 67.5 us  [the longest x5 51.5 us: spread(): return lax.all_to_all(copies, axis, 0, 0, tiled=True)]
    all_gather x1 -> x0, blocking collectives: 46.5 us -> none  [on_device(): lax.all_gather(q_start, 'fsdp', axis=1, tiled=True)]
    all_to_all x0 -> x2, waiting for transfers between devices: none -> 33.6 us  [the longest x1 27.7 us: on_device(): lax.all_to_all(blocks, CHIP, 0, 0, tiled=True).reshape(chips * rows, width)]
    all_to_all x0 -> x2, starting transfers between devices: none -> 8.15 us  [the longest x1 4.41 us: on_device(): lax.all_to_all(blocks, CHIP, 0, 0, tiled=True).reshape(chips * rows, width)]
    ppermute x0 -> x7, waiting for transfers between devices: none -> 6.62 us  [swap_cores(): return lax.ppermute(values, 'core', SWAP)]
    dot_general x7 -> x11, matrix products: 9.32 us -> 10.9 us  [the longest x2 3.81 us: transposed_product(): lax.dot_general(left, right, (((0,), (0,)), ((), ())), preferred_element_...]
  transfers between devices with their start and end apart: 1 -> 9, of which waited for: 1 -> 9; matrix products, arithmetic and copies ran while one was open for 0% -> 9% of each run, Pallas kernels for 0% -> 0%
where the time goes in v1:
time: 155 us; the launch traced here: 154 us
  blocking collectives  67.5 us (44%)
  waiting for transfers between devices  40.2 us (26%)
  other arithmetic  17.1 us (11%)
  matrix products  11.4 us (7%)
  starting transfers between devices  9.23 us (6%)
  local copies, waits for them, and re-layouts  8.08 us (5%)
    all_to_all x5, blocking collectives, spread(): return lax.all_to_all(copies, axis, 0, 0, tiled=True)  51.5 us
    all_to_all x1, waiting for transfers between devices, on_device(): lax.all_to_all(blocks, CHIP, 0, 0, tiled=True).reshape(chips * rows, width)  27.7 us
    all_to_all x1, blocking collectives, on_device(): p_own = jnp.sum(lax.all_to_all(term, CHIP, 0, 0, tiled=True), axis=0)  16 us
    another operation x6, other arithmetic, orthonormal_basis(): factor = jnp.linalg.cholesky(gram_matrix)  7.19 us
    ppermute x7, waiting for transfers between devices, swap_cores(): return lax.ppermute(values, 'core', SWAP)  6.62 us
    another operation x4, other arithmetic, orthonormal_basis(): lax.linalg.triangular_solve(factor, jnp.eye(factor.shape[0], dtype=jnp.fl...  6.17 us
    all_to_all x1, waiting for transfers between devices, spread(): return lax.all_to_all(copies, axis, 0, 0, tiled=True)  5.9 us
    all_to_all x1, starting transfers between devices, on_device(): lax.all_to_all(blocks, CHIP, 0, 0, tiled=True).reshape(chips * rows, width)  4.41 us
  transfers between devices with their start and end apart: 9, of which 9 were waited for; matrix products, arithmetic and copies ran while one was open for 9% of the time, Pallas kernels for 0%

profile of v1, /device:TPU:0, one launch (start us, length us, event | category | flops | bytes accessed | tf_op | source)
XLA Modules:
  0.0 154.5 jit_solution(14099922741058444311)
XLA Ops:
  0.6 0.7 constant_dynamic-slice_fusion.3
  1.4 0.5 collective-permute-start
  1.9 0.8 collective-permute-done
  2.7 0.7 broadcast_select_fusion.1
  3.5 12.0 %all_to_all.40 = bf16[4,16,896]{2,1,0:T(8,128)(2,1)S(1)} all-to-all(bf16[4,16,896]{2,1,0:T(8,128)(2,1)S(1)} %broadcast_in_dim.15), channel_id=1, replica_groups=mesh['rep'=1,'hi'=4,'lo'=4,'core'=2] {'hi'}, dimensions={0} | all-to-all | bytes 229376 | tf_op jit(solution)/shard_map/all_to_all | solution.py:27
  15.6 0.1 broadcast_in_dim.16
  15.7 10.6 %all_to_all.41 = bf16[4,4,16,896]{3,1,2,0:T(4,128)(2,1)S(1)} all-to-all(bf16[4,4,16,896]{3,1,2,0:T(4,128)(2,1)S(1)} %broadcast_in_dim.16), channel_id=1, replica_groups=mesh['rep'=1,'hi'=4,'lo'=4,'core'=2] {'lo'}, dimensions={0} | all-to-all | bytes 917504 | tf_op jit(solution)/shard_map/all_to_all | solution.py:27
  26.3 0.4 copy.29
  26.7 0.3 reshape.69
  27.1 0.6 fusion.6
  27.7 1.2 collective-permute-done.1
  28.9 0.6 fusion.9
  29.5 0.8 reshape.83
  30.3 3.7 %all-to-all-start.2 = ((f32[16,1,2048]{2,1,0:T(1,128)}), f32[16,1,2048]{2,1,0:T(1,128)S(1)}, u32[]{:S(2)}, u32[]{:S(2)}) async-start(f32[16,1,2048]{2,1,0:T(1,128)} %reshape.83), calls=%async_computation.2 | async-start | bytes 262144 | tf_op jit(solution)/shard_map/all_to_all | solution.py:27
  34.1 0.2 copy.48
  34.3 1.6 %copy.34 = bf16[16,64,896]{2,1,0:T(8,128)(2,1)} copy(bf16[16,64,896]{2,0,1:T(8,128)(2,1)S(1)} %bitcast.87) | data formatting | bytes 3670016 | tf_op jit(solution)/shard_map/transpose | solution.py:63
  36.0 5.9 %all-to-all-done.2 = f32[16,1,2048]{2,1,0:T(1,128)S(1)} async-done(((f32[16,1,2048]{2,1,0:T(1,128)}), f32[16,1,2048]{2,1,0:T(1,128)S(1)}, u32[]{:S(2)}, u32[]{:S(2)}) %all-to-all-start.2) | async-done | bytes 131104 | tf_op jit(solution)/shard_map/all_to_all | solution.py:27
  41.9 4.4 %all-to-all-start.3 = ((bf16[16,64,896]{2,1,0:T(8,128)(2,1)}), bf16[16,64,896]{2,1,0:T(8,128)(2,1)}, u32[]{:S(2)}, u32[]{:S(2)}) async-start(bf16[16,64,896]{2,1,0:T(8,128)(2,1)} %copy.34), calls=%async_computation.3 | async-start | bytes 3670016 | tf_op jit(solution)/shard_map/all_to_all | solution.py:64
  46.3 0.5 broadcast.45
  46.8 0.9 reduce.4
  47.8 0.1 reshape.84
  47.9 0.3 convolution_bitcast_fusion.2
  48.3 0.2 copy.30
  48.5 0.1 reshape.70
  48.6 0.9 collective-permute-done.2
  49.6 2.9 %cholesky.44 = f32[32,32]{1,0:T(8,128)S(1)} custom-call(f32[32,32]{1,0:T(8,128)S(1)} %fusion.24), custom_call_target="Cholesky" | custom-call | tf_op jit(solution)/shard_map/jit(cholesky)/cholesky | solution.py:45
  52.5 0.6 compare_reduce_fusion.1
  53.2 0.7 fusion.19
  53.8 2.4 %custom-call.6 = f32[1,32,32]{1,2,0:T(8,128)S(1)} custom-call(f32[1,32,32]{2,1,0:T(8,128)S(1)} %fusion.19), custom_call_target="InvertDiagBlocksLowerTriangular" | custom-call | tf_op jit(solution)/shard_map/triangular_solve/custom-call.0 | solution.py:46
  56.3 0.2 fusion.17
  56.5 0.2 convolution_convert_fusion.1
  56.8 27.7 %all-to-all-done.3 = bf16[16,64,896]{2,1,0:T(8,128)(2,1)} async-done(((bf16[16,64,896]{2,1,0:T(8,128)(2,1)}), bf16[16,64,896]{2,1,0:T(8,128)(2,1)}, u32[]{:S(2)}, u32[]{:S(2)}) %all-to-all-start.3) | async-done | bytes 1835040 | tf_op jit(solution)/shard_map/all_to_all | solution.py:64
  84.4 1.9 %fusion.32 = f32[32,896]{1,0:T(8,128)S(1)} fusion(bf16[1024,32]{0,1:T(8,128)(2,1)S(1)} %convolution_convert_fusion.1, bf16[1024,896]{1,0:T(8,128)(2,1)} %bitcast.11), kind=kOutput, calls=%fused_computation.58 | convolution fusion | flops 58720256 | bytes 2015232 | tf_op jit(solution)/shard_map/dot_general | solution.py:14
  86.4 1.3 collective-permute-done.3
  87.7 2.1 %convolution_bitcast_fusion = f32[1024,32]{0,1:T(8,128)S(1)} fusion(bf16[1024,896]{1,0:T(8,128)(2,1)} %bitcast.11, f32[32,896]{1,0:T(8,128)S(1)} %fusion.32, f32[32,896]{1,0:T(8,128)S(1)} %collective-permute-done.3), kind=kOutput, calls=%fused_computation.7 | convolution fusion | flops 58777600 | bytes 2195456 | tf_op jit(solution)/shard_map/dot_general | solution.py:18
  89.9 0.1 reshape.72
  90.1 0.2 reshape.85
  90.3 16.0 %all_to_all.42 = f32[16,1,2048]{2,1,0:T(1,128)S(1)} all-to-all(f32[16,1,2048]{2,1,0:T(1,128)S(1)} %reshape.85), channel_id=1, replica_groups=mesh['rep'=1,'hi'=4,'lo'=4,'core'=2] {'hi','lo'}, dimensions={0} | all-to-all | bytes 262144 | tf_op jit(solution)/shard_map/all_to_all | solution.py:82
  106.3 0.9 reduce.5
  107.4 0.2 reshape.87
  107.6 10.7 %all_to_all.43 = f32[16,1,2048]{2,1,0:T(1,128)S(1)} all-to-all(f32[16,1,2048]{2,1,0:T(1,128)S(1)} %reshape.87), channel_id=1, replica_groups=mesh['rep'=1,'hi'=4,'lo'=4,'core'=2] {'hi','lo'}, dimensions={0} | all-to-all | bytes 262144 | tf_op jit(solution)/shard_map/all_to_all | solution.py:27
  118.3 0.9 reduce.6
  119.4 0.3 convolution_bitcast_fusion.1
  119.8 0.2 copy.39
  120.0 0.1 reshape.73
  120.1 0.9 collective-permute-done.4
  121.1 2.9 %cholesky.55 = f32[32,32]{1,0:T(8,128)S(1)} custom-call(f32[32,32]{1,0:T(8,128)S(1)} %fusion.22), custom_call_target="Cholesky" | custom-call | tf_op jit(solution)/shard_map/jit(cholesky)/cholesky | solution.py:45
  124.0 0.6 compare_reduce_fusion
  124.7 0.7 fusion.20
  125.3 2.4 %custom-call.7 = f32[1,32,32]{1,2,0:T(8,128)S(1)} custom-call(f32[1,32,32]{2,1,0:T(8,128)S(1)} %fusion.20), custom_call_target="InvertDiagBlocksLowerTriangular" | custom-call | tf_op jit(solution)/shard_map/triangular_solve/custom-call.0 | solution.py:46
  127.7 0.2 fusion.15
  128.0 0.2 convolution_convert_fusion
  128.2 1.9 %fusion.33 = f32[32,896]{1,0:T(8,128)S(1)} fusion(bf16[1024,32]{0,1:T(8,128)(2,1)S(1)} %convolution_convert_fusion, bf16[1024,896]{1,0:T(8,128)(2,1)} %bitcast.11), kind=kOutput, calls=%fused_computation.59 | convolution fusion | flops 58720256 | bytes 2015232 | tf_op jit(solution)/shard_map/dot_general | solution.py:14
  130.2 0.2 collective-permute-start.5
  130.4 1.2 collective-permute-done.5
  131.6 8.6 %all_to_all.44 = bf16[4,16,896]{2,1,0:T(8,128)(2,1)S(1)} all-to-all(bf16[4,16,896]{2,1,0:T(8,128)(2,1)S(1)} %broadcast_in_dim.19), channel_id=1, replica_groups=mesh['rep'=1,'hi'=4,'lo'=4,'core'=2] {'hi'}, dimensions={0} | all-to-all | bytes 229376 | tf_op jit(solution)/shard_map/all_to_all | solution.py:27
  140.2 0.1 broadcast_in_dim.20
  140.4 9.6 %all_to_all.45 = bf16[4,4,16,896]{3,1,2,0:T(4,128)(2,1)S(1)} all-to-all(bf16[4,4,16,896]{3,1,2,0:T(4,128)(2,1)S(1)} %broadcast_in_dim.20), channel_id=1, replica_groups=mesh['rep'=1,'hi'=4,'lo'=4,'core'=2] {'lo'}, dimensions={0} | all-to-all | bytes 917504 | tf_op jit(solution)/shard_map/all_to_all | solution.py:27
  150.0 0.4 copy.41
  150.3 0.3 reshape.74
  150.8 0.8 fusion.29
  151.5 0.7 constant_dynamic-slice_fusion
  152.2 0.3 collective-permute-done.6
  152.6 1.9 %fusion.1 = bf16[1,64,14336]{2,1,0:T(8,128)(2,1)} fusion(bf16[1,64,14336]{2,1,0:T(8,128)(2,1)S(1)} %copy-done, bf16[16,14336]{1,0:T(8,128)(2,1)S(1)} %collective-permute-done.6, bf16[16,14336]{1,0:T(8,128)(2,1)S(1)} %reshape.74, bf16[64,16]{0,1:T(8,128)(2,1)S(1)} %get-tuple-element.8, bf16[64,16]{0,1:T(8,128)(2,1)S(1)} %get-tuple-element.7), kind=kOutput, calls=%fused_computation.2 | convolution fusion | flops 63315968 | bytes 4591616 | tf_op jit(solution)/shard_map/dot_general | solution.py:98
  (30 shorter events, 1.2 us)
Async XLA Ops:
  1.4 1.3 collective-permute-start
  15.5 11.6 %copy-start = (bf16[1,64,14336]{2,1,0:T(8,128)(2,1)S(1)}, bf16[1,64,14336]{2,1,0:T(8,128)(2,1)}, u32[]{:S(2)}) copy-start(bf16[1,64,14336]{2,1,0:T(8,128)(2,1)} %param.5) | copy-start | bytes 5505028
  27.0 1.9 %collective-permute-start.1 = (bf16[16,14336]{1,0:T(8,128)(2,1)S(1)}, bf16[16,14336]{1,0:T(8,128)(2,1)S(1)}, u32[]{:S(2)}, u32[]{:S(2)}) collective-permute-start(bf16[16,14336]{1,0:T(8,128)(2,1)S(1)} %reshape.69), channel_id=1, source_target_pairs={{0,1},{1,0},{2,3},{3,2},{4,5},{5,4},{6,7},{7,6},{8,9},{9,8},{10,11... | collective-permute-start | bytes 1376264 | tf_op jit(solution)/shard_map/ppermute | solution.py:22
  30.3 11.5 %all-to-all-start.2 = ((f32[16,1,2048]{2,1,0:T(1,128)}), f32[16,1,2048]{2,1,0:T(1,128)S(1)}, u32[]{:S(2)}, u32[]{:S(2)}) async-start(f32[16,1,2048]{2,1,0:T(1,128)} %reshape.83), calls=%async_computation.2 | async-start | bytes 262144 | tf_op jit(solution)/shard_map/all_to_all | solution.py:27
  41.9 42.5 %all-to-all-start.3 = ((bf16[16,64,896]{2,1,0:T(8,128)(2,1)}), bf16[16,64,896]{2,1,0:T(8,128)(2,1)}, u32[]{:S(2)}, u32[]{:S(2)}) async-start(bf16[16,64,896]{2,1,0:T(8,128)(2,1)} %copy.34), calls=%async_computation.3 | async-start | bytes 3670016 | tf_op jit(solution)/shard_map/all_to_all | solution.py:64
  48.2 1.2 collective-permute-start.2
  86.3 1.4 collective-permute-start.3
  119.7 1.2 collective-permute-start.4
  130.2 1.4 collective-permute-start.5
  150.7 1.9 %collective-permute-start.6 = (bf16[16,14336]{1,0:T(8,128)(2,1)S(1)}, bf16[16,14336]{1,0:T(8,128)(2,1)S(1)}, u32[]{:S(2)}, u32[]{:S(2)}) collective-permute-start(bf16[16,14336]{1,0:T(8,128)(2,1)S(1)} %reshape.74), channel_id=1, source_target_pairs={{0,1},{1,0},{2,3},{3,2},{4,5},{5,4},{6,7},{7,6},{8,9},{9,8},{10,11... | collective-permute-start | bytes 1376264 | tf_op jit(solution)/shard_map/ppermute | solution.py:22

commit v2 on v1

--- a/solution.py
+++ b/solution.py
@@ -2,6 +2,7 @@
 import jax.numpy as jnp
 from jax import lax
 from jax.sharding import Mesh, PartitionSpec as P
+
 
 ITERS = 2
 HIGHEST = lax.Precision.HIGHEST
@@ -27,13 +28,34 @@
     return lax.all_to_all(copies, axis, 0, 0, tiled=True)
 
 
+def doubled(values, axis, dim):
+    values = jnp.expand_dims(values, dim)
+    position = lax.axis_index(axis)
+    size = lax.axis_size(axis)
+    bit = 1
+    while bit < size:
+        pairs = tuple((index, index ^ bit) for index in range(size))
+        taken = lax.ppermute(values, axis, pairs)
+        upper = (position & bit) != 0
+        values = jnp.where(
+            upper,
+            jnp.concatenate([taken, values], axis=dim),
+            jnp.concatenate([values, taken], axis=dim),
+        )
+        bit *= 2
+    return values
+
+
 def gather_chips(values):
     by_hi = spread(values, "hi")
     return spread(by_hi, "lo").swapaxes(0, 1)
 
 
-def gather_right(q_half):
-    blocks = gather_chips(q_half)
+def gather_right(q_half, in_pairs):
+    if in_pairs:
+        blocks = doubled(doubled(q_half, "hi", 0), "lo", 1)
+    else:
+        blocks = gather_chips(q_half)
     hi, lo, half, width = blocks.shape
     own = blocks.transpose(2, 0, 1, 3).reshape(half, hi * lo * width)
     return own, swap_cores(own)
@@ -68,7 +90,7 @@
     taken = swap_cores(given)
     first = jnp.where(core == 0, kept, taken)
     second = jnp.where(core == 0, taken, kept)
-    own, other = gather_right(jnp.concatenate([first, second], axis=1))
+    own, other = gather_right(jnp.concatenate([first, second], axis=1), True)
     p_mine = product_transposed(own_rows, own)
     p_theirs = product_transposed(own_rows, other)
     p_own = jnp.where(
@@ -82,7 +104,10 @@
             p_own = jnp.sum(lax.all_to_all(term, CHIP, 0, 0, tiled=True), axis=0)
         if replicas > 1:
             p_own = lax.psum(p_own, "rep")
-        p_rows = spread(p_own, CHIP).reshape(chips * rows, rank)
+        if iteration > 0:
+            p_rows = spread(p_own, CHIP).reshape(chips * rows, rank)
+        else:
+            p_rows = doubled(doubled(p_own, "hi", 0), "lo", 1).reshape(chips * rows, rank)
         basis, basis_own = orthonormal_basis(p_rows, p_own)
         q_term = transposed_product(basis.astype(jnp.bfloat16), block)
         q_chip = q_term + swap_cores(q_term)
@@ -91,7 +116,7 @@
         q_chip = q_chip / replicas
         right_factor = q_chip.astype(jnp.bfloat16)
     q_owned = lax.dynamic_slice_in_dim(q_chip, core * shard_cols, shard_cols, 1)
-    own, other = gather_right(lax.dynamic_slice_in_dim(right_factor, core * half, half, 0))
+    own, other = gather_right(lax.dynamic_slice_in_dim(right_factor, core * half, half, 0), False)
     basis_bf16 = basis_own.astype(jnp.bfloat16)
     mine = lax.dynamic_slice_in_dim(basis_bf16, core * half, half, 1)
     theirs = lax.dynamic_slice_in_dim(basis_bf16, (1 - core) * half, half, 1)

time: 155 us -> 170 us (1.097)
  waiting for transfers between devices: 40.2 us -> 70.6 us
  blocking collectives: 67.5 us -> 40.9 us
  starting transfers between devices: 9.23 us -> 20.2 us
    ppermute x0 -> x8, waiting for transfers between devices: none -> 64.2 us  [doubled(): taken = lax.ppermute(values, axis, pairs)]
    all_to_all x1, waiting for transfers between devices: 27.7 us -> 0.01 us  [on_device(): lax.all_to_all(blocks, CHIP, 0, 0, tiled=True).reshape(chips * rows, width)]
    all_to_all x5 -> x3, blocking collectives: 51.5 us -> 28.9 us  [spread(): return lax.all_to_all(copies, axis, 0, 0, tiled=True)]
    ppermute x0 -> x8, starting transfers between devices: none -> 13 us  [doubled(): taken = lax.ppermute(values, axis, pairs)]
    all_to_all x1 -> x0, waiting for transfers between devices: 5.9 us -> none  [spread(): return lax.all_to_all(copies, axis, 0, 0, tiled=True)]
    all_to_all x1, blocking collectives: 16 us -> 12 us  [on_device(): p_own = jnp.sum(lax.all_to_all(term, CHIP, 0, 0, tiled=True), axis=0)]
    all_to_all x1 -> x0, starting transfers between devices: 3.73 us -> none  [spread(): return lax.all_to_all(copies, axis, 0, 0, tiled=True)]
  transfers between devices with their start and end apart: 9 -> 16, of which waited for: 9 -> 14; matrix products, arithmetic and copies ran while one was open for 9% -> 9% of each run, Pallas kernels for 0% -> 0%
where the time goes in v2:
time: 170 us; the launch traced here: 169 us
  waiting for transfers between devices  70.6 us (42%)
  blocking collectives  40.9 us (24%)
  starting transfers between devices  20.2 us (12%)
  other arithmetic  16.4 us (10%)
  matrix products  11.4 us (7%)
  local copies, waits for them, and re-layouts  8.56 us (5%)
    ppermute x8, waiting for transfers between devices, doubled(): taken = lax.ppermute(values, axis, pairs)  64.2 us
    all_to_all x3, blocking collectives, spread(): return lax.all_to_all(copies, axis, 0, 0, tiled=True)  28.9 us
    ppermute x8, starting transfers between devices, doubled(): taken = lax.ppermute(values, axis, pairs)  13 us
    all_to_all x1, blocking collectives, on_device(): p_own = jnp.sum(lax.all_to_all(term, CHIP, 0, 0, tiled=True), axis=0)  12 us
    another operation x6, other arithmetic, orthonormal_basis(): factor = jnp.linalg.cholesky(gram_matrix)  7.19 us
    ppermute x7, waiting for transfers between devices, swap_cores(): return lax.ppermute(values, 'core', SWAP)  6.34 us
    another operation x4, other arithmetic, orthonormal_basis(): lax.linalg.triangular_solve(factor, jnp.eye(factor.shape[0], dtype=jnp.fl...  6.17 us
    all_to_all x1, starting transfers between devices, on_device(): lax.all_to_all(blocks, CHIP, 0, 0, tiled=True).reshape(chips * rows, width)  5.9 us
  transfers between devices with their start and end apart: 16, of which 14 were waited for; matrix products, arithmetic and copies ran while one was open for 9% of the time, Pallas kernels for 0%

profile of v2, /device:TPU:0, one launch (start us, length us, event | category | flops | bytes accessed | tf_op | source)
XLA Modules:
  0.0 169.0 jit_solution(1437935036130445000)
XLA Ops:
  0.6 0.7 constant_dynamic-slice_fusion.3
  1.4 0.5 collective-permute-start
  1.9 0.8 collective-permute-done
  2.7 0.7 broadcast_select_fusion.1
  3.5 2.9 %collective-permute-start.1 = (bf16[1,16,896]{2,1,0:T(8,128)(2,1)S(1)}, bf16[1,16,896]{2,1,0:T(8,128)(2,1)S(1)}, u32[]{:S(2)}, u32[]{:S(2)}) collective-permute-start(bf16[1,16,896]{2,1,0:T(8,128)(2,1)S(1)} %maximum_bitcast_fusion), channel_id=1, source_target_pairs={{0,8},{8,0},{16,24},{24,16},{1,9},{9,1},{17,25},{25,17},{2,10},{10... | collective-permute-start | bytes 86024 | tf_op jit(solution)/shard_map/ppermute | solution.py:38
  6.4 1.7 %copy.57 = bf16[8,8,16,896]{3,2,1,0:T(8,128)(2,1)S(1)} copy(bf16[8,8,16,896]{3,1,2,0:T(8,128)(2,1)} %bitcast.94) | data formatting | bytes 3670016
  8.2 1.6 copy.43
  9.8 5.9 %all-to-all-start = ((bf16[16,64,896]{2,1,0:T(8,128)(2,1)}), bf16[16,64,896]{2,1,0:T(8,128)(2,1)}, u32[]{:S(2)}, u32[]{:S(2)}) async-start(bf16[16,64,896]{2,1,0:T(8,128)(2,1)} %copy.43), calls=%async_computation | async-start | bytes 3670016 | tf_op jit(solution)/shard_map/all_to_all | solution.py:86
  15.8 2.8 %collective-permute-start.2 = (bf16[2,16,896]{2,1,0:T(8,128)(2,1)S(1)}, bf16[2,16,896]{2,1,0:T(8,128)(2,1)S(1)}, u32[]{:S(2)}, u32[]{:S(2)}) collective-permute-start(bf16[2,16,896]{2,1,0:T(8,128)(2,1)S(1)} %maximum_select_fusion.6), channel_id=1, source_target_pairs={{0,16},{8,24},{16,0},{24,8},{1,17},{9,25},{17,1},{25,9},{2,18},{10... | collective-permute-start | bytes 172040 | tf_op jit(solution)/shard_map/ppermute | solution.py:38
  18.6 42.1 %collective-permute-done.2 = bf16[2,16,896]{2,1,0:T(8,128)(2,1)S(1)} collective-permute-done((bf16[2,16,896]{2,1,0:T(8,128)(2,1)S(1)}, bf16[2,16,896]{2,1,0:T(8,128)(2,1)S(1)}, u32[]{:S(2)}, u32[]{:S(2)}) %collective-permute-start.2) | collective-permute-done | bytes 57376 | tf_op jit(solution)/shard_map/ppermute | solution.py:38
  60.8 1.5 collective-permute-start.3
  62.3 3.3 %collective-permute-done.3 = bf16[4,1,16,896]{3,2,0,1:T(8,128)(2,1)S(1)} collective-permute-done((bf16[4,1,16,896]{3,2,0,1:T(8,128)(2,1)S(1)}, bf16[4,1,16,896]{3,2,0,1:T(8,128)(2,1)S(1)}, u32[]{:S(2)}, u32[]{:S(2)}) %collective-permute-start.3) | collective-permute-done | bytes 114720 | tf_op jit(solution)/shard_map/ppermute | solution.py:38
  65.7 2.6 %collective-permute-start.4 = (bf16[4,2,16,896]{3,2,0,1:T(8,128)(2,1)S(1)}, bf16[4,2,16,896]{3,2,0,1:T(8,128)(2,1)S(1)}, u32[]{:S(2)}, u32[]{:S(2)}) collective-permute-start(bf16[4,2,16,896]{3,2,0,1:T(8,128)(2,1)S(1)} %maximum_select_fusion.2), channel_id=1, source_target_pairs={{0,4},{2,6},{4,0},{6,2},{1,5},{3,7},{5,1},{7,3},{8,12},{10,14},{12... | collective-permute-start | bytes 688136 | tf_op jit(solution)/shard_map/ppermute | solution.py:38
  68.2 4.0 %collective-permute-done.4 = bf16[4,2,16,896]{3,2,0,1:T(8,128)(2,1)S(1)} collective-permute-done((bf16[4,2,16,896]{3,2,0,1:T(8,128)(2,1)S(1)}, bf16[4,2,16,896]{3,2,0,1:T(8,128)(2,1)S(1)}, u32[]{:S(2)}, u32[]{:S(2)}) %collective-permute-start.4) | collective-permute-done | bytes 229408 | tf_op jit(solution)/shard_map/ppermute | solution.py:38
  72.3 0.4 copy.36
  72.7 0.3 reshape.307
  73.1 0.6 fusion.6
  73.7 1.2 collective-permute-done.5
  74.9 0.6 fusion.9
  75.6 3.7 %collective-permute-done.6 = f32[1,64,32]{1,2,0:T(8,128)S(1)} collective-permute-done((f32[1,64,32]{1,2,0:T(8,128)S(1)}, f32[1,64,32]{1,2,0:T(8,128)S(1)}, u32[]{:S(2)}, u32[]{:S(2)}) %collective-permute-start.6) | collective-permute-done | bytes 8224 | tf_op jit(solution)/shard_map/ppermute | solution.py:38
  79.3 4.8 %collective-permute-done.7 = f32[2,64,32]{1,2,0:T(8,128)S(1)} collective-permute-done((f32[2,64,32]{1,2,0:T(8,128)S(1)}, f32[2,64,32]{1,2,0:T(8,128)S(1)}, u32[]{:S(2)}, u32[]{:S(2)}) %collective-permute-start.7) | collective-permute-done | bytes 16416 | tf_op jit(solution)/shard_map/ppermute | solution.py:38
  84.1 1.0 collective-permute-start.8
  85.2 3.3 %collective-permute-done.8 = f32[4,1,64,32]{2,3,0,1:T(8,128)S(1)} collective-permute-done((f32[4,1,64,32]{2,3,0,1:T(8,128)S(1)}, f32[4,1,64,32]{2,3,0,1:T(8,128)S(1)}, u32[]{:S(2)}, u32[]{:S(2)}) %collective-permute-start.8) | collective-permute-done | bytes 32800 | tf_op jit(solution)/shard_map/ppermute | solution.py:38
  88.5 2.1 %collective-permute-start.9 = (f32[4,2,64,32]{2,3,0,1:T(8,128)S(1)}, f32[4,2,64,32]{2,3,0,1:T(8,128)S(1)}, u32[]{:S(2)}, u32[]{:S(2)}) collective-permute-start(f32[4,2,64,32]{2,3,0,1:T(8,128)S(1)} %maximum_select_fusion.3), channel_id=1, source_target_pairs={{0,4},{2,6},{4,0},{6,2},{1,5},{3,7},{5,1},{7,3},{8,12},{10,14},{12... | collective-permute-start | bytes 196616 | tf_op jit(solution)/shard_map/ppermute | solution.py:38
  90.5 2.9 %collective-permute-done.9 = f32[4,2,64,32]{2,3,0,1:T(8,128)S(1)} collective-permute-done((f32[4,2,64,32]{2,3,0,1:T(8,128)S(1)}, f32[4,2,64,32]{2,3,0,1:T(8,128)S(1)}, u32[]{:S(2)}, u32[]{:S(2)}) %collective-permute-start.9) | collective-permute-done | bytes 65568 | tf_op jit(solution)/shard_map/ppermute | solution.py:38
  93.5 0.3 convolution_bitcast_fusion.2
  94.1 0.2 select_n.165
  94.4 0.8 collective-permute-done.10
  95.2 2.9 %cholesky.44 = f32[32,32]{1,0:T(8,128)S(1)} custom-call(f32[32,32]{1,0:T(8,128)S(1)} %fusion.26), custom_call_target="Cholesky" | custom-call | tf_op jit(solution)/shard_map/jit(cholesky)/cholesky | solution.py:67
  98.2 0.6 compare_reduce_fusion.1
  98.8 0.7 fusion.21
  99.5 2.4 %custom-call.6 = f32[1,32,32]{1,2,0:T(8,128)S(1)} custom-call(f32[1,32,32]{2,1,0:T(8,128)S(1)} %fusion.21), custom_call_target="InvertDiagBlocksLowerTriangular" | custom-call | tf_op jit(solution)/shard_map/triangular_solve/custom-call.0 | solution.py:68
  101.9 0.2 fusion.19
  102.1 0.2 convolution_convert_fusion.1
  102.4 1.9 %fusion.33 = f32[32,896]{1,0:T(8,128)S(1)} fusion(bf16[1024,32]{0,1:T(8,128)(2,1)S(1)} %convolution_convert_fusion.1, bf16[1024,896]{1,0:T(8,128)(2,1)} %bitcast.20), kind=kOutput, calls=%fused_computation.66 | convolution fusion | flops 58720256 | bytes 2015232 | tf_op jit(solution)/shard_map/dot_general | solution.py:15
  104.3 0.2 collective-permute-start.11
  104.6 1.2 collective-permute-done.11
  105.7 2.1 %convolution_bitcast_fusion = f32[1024,32]{0,1:T(8,128)S(1)} fusion(bf16[1024,896]{1,0:T(8,128)(2,1)} %bitcast.20, f32[32,896]{1,0:T(8,128)S(1)} %fusion.33, f32[32,896]{1,0:T(8,128)S(1)} %collective-permute-done.11), kind=kOutput, calls=%fused_computation.7 | convolution fusion | flops 58777600 | bytes 2195456 | tf_op jit(solution)/shard_map/dot_general | solution.py:19
  108.1 0.2 reshape.320
  108.2 12.0 %all_to_all.25 = f32[16,1,2048]{2,1,0:T(1,128)S(1)} all-to-all(f32[16,1,2048]{2,1,0:T(1,128)S(1)} %reshape.320), channel_id=1, replica_groups=mesh['rep'=1,'hi'=4,'lo'=4,'core'=2] {'hi','lo'}, dimensions={0} | all-to-all | bytes 262144 | tf_op jit(solution)/shard_map/all_to_all | solution.py:104
  120.3 0.5 broadcast.81
  120.8 0.9 reduce.4
  121.9 0.2 reshape.322
  122.1 10.7 %all_to_all.26 = f32[16,1,2048]{2,1,0:T(1,128)S(1)} all-to-all(f32[16,1,2048]{2,1,0:T(1,128)S(1)} %reshape.322), channel_id=1, replica_groups=mesh['rep'=1,'hi'=4,'lo'=4,'core'=2] {'hi','lo'}, dimensions={0} | all-to-all | bytes 262144 | tf_op jit(solution)/shard_map/all_to_all | solution.py:28
  132.8 0.9 reduce.5
  133.9 0.3 convolution_bitcast_fusion.1
  134.6 0.9 collective-permute-done.12
  135.6 2.9 %cholesky.55 = f32[32,32]{1,0:T(8,128)S(1)} custom-call(f32[32,32]{1,0:T(8,128)S(1)} %fusion.24), custom_call_target="Cholesky" | custom-call | tf_op jit(solution)/shard_map/jit(cholesky)/cholesky | solution.py:67
  138.5 0.6 compare_reduce_fusion
  139.2 0.7 fusion.22
  139.8 2.4 %custom-call.7 = f32[1,32,32]{1,2,0:T(8,128)S(1)} custom-call(f32[1,32,32]{2,1,0:T(8,128)S(1)} %fusion.22), custom_call_target="InvertDiagBlocksLowerTriangular" | custom-call | tf_op jit(solution)/shard_map/triangular_solve/custom-call.0 | solution.py:68
  142.3 0.2 fusion.17
  142.5 0.2 convolution_convert_fusion
  142.7 1.9 %fusion.34 = f32[32,896]{1,0:T(8,128)S(1)} fusion(bf16[1024,32]{0,1:T(8,128)(2,1)S(1)} %convolution_convert_fusion, bf16[1024,896]{1,0:T(8,128)(2,1)} %bitcast.20), kind=kOutput, calls=%fused_computation.67 | convolution fusion | flops 58720256 | bytes 2015232 | tf_op jit(solution)/shard_map/dot_general | solution.py:15
  144.7 0.2 collective-permute-start.13
  144.9 1.2 collective-permute-done.13
  146.1 8.6 %all_to_all.27 = bf16[4,16,896]{2,1,0:T(8,128)(2,1)S(1)} all-to-all(bf16[4,16,896]{2,1,0:T(8,128)(2,1)S(1)} %broadcast_in_dim.13), channel_id=1, replica_groups=mesh['rep'=1,'hi'=4,'lo'=4,'core'=2] {'hi'}, dimensions={0} | all-to-all | bytes 229376 | tf_op jit(solution)/shard_map/all_to_all | solution.py:28
  154.9 9.6 %all_to_all.28 = bf16[4,4,16,896]{3,1,2,0:T(4,128)(2,1)S(1)} all-to-all(bf16[4,4,16,896]{3,1,2,0:T(4,128)(2,1)S(1)} %broadcast_in_dim.14), channel_id=1, replica_groups=mesh['rep'=1,'hi'=4,'lo'=4,'core'=2] {'lo'}, dimensions={0} | all-to-all | bytes 917504 | tf_op jit(solution)/shard_map/all_to_all | solution.py:28
  164.5 0.4 copy.50
  164.8 0.3 reshape.311
  165.3 0.8 fusion.31
  166.0 0.7 constant_dynamic-slice_fusion
  166.7 0.3 collective-permute-done.14
  167.1 1.9 %fusion.1 = bf16[1,64,14336]{2,1,0:T(8,128)(2,1)} fusion(bf16[1,64,14336]{2,1,0:T(8,128)(2,1)S(1)} %copy-done, bf16[16,14336]{1,0:T(8,128)(2,1)S(1)} %collective-permute-done.14, bf16[16,14336]{1,0:T(8,128)(2,1)S(1)} %reshape.311, bf16[64,16]{0,1:T(8,128)(2,1)S(1)} %get-tuple-element.8, bf16[64,16]{0,1:T(8,128)(2,1)S(1)} %get-tuple-element.7), kind=kOutput, calls=%fused_computation.2 | convolution fusion | flops 63315968 | bytes 4591616 | tf_op jit(solution)/shard_map/dot_general | solution.py:123
  (45 shorter events, 2.0 us)
Async XLA Ops:
  1.4 1.3 collective-permute-start
  3.5 12.2 %collective-permute-start.1 = (bf16[1,16,896]{2,1,0:T(8,128)(2,1)S(1)}, bf16[1,16,896]{2,1,0:T(8,128)(2,1)S(1)}, u32[]{:S(2)}, u32[]{:S(2)}) collective-permute-start(bf16[1,16,896]{2,1,0:T(8,128)(2,1)S(1)} %maximum_bitcast_fusion), channel_id=1, source_target_pairs={{0,8},{8,0},{16,24},{24,16},{1,9},{9,1},{17,25},{25,17},{2,10},{10... | collective-permute-start | bytes 86024 | tf_op jit(solution)/shard_map/ppermute | solution.py:38
  9.8 92.6 %all-to-all-start = ((bf16[16,64,896]{2,1,0:T(8,128)(2,1)}), bf16[16,64,896]{2,1,0:T(8,128)(2,1)}, u32[]{:S(2)}, u32[]{:S(2)}) async-start(bf16[16,64,896]{2,1,0:T(8,128)(2,1)} %copy.43), calls=%async_computation | async-start | bytes 3670016 | tf_op jit(solution)/shard_map/all_to_all | solution.py:86
  15.7 57.4 %copy-start = (bf16[1,64,14336]{2,1,0:T(8,128)(2,1)S(1)}, bf16[1,64,14336]{2,1,0:T(8,128)(2,1)}, u32[]{:S(2)}) copy-start(bf16[1,64,14336]{2,1,0:T(8,128)(2,1)} %param.5) | copy-start | bytes 5505028
  15.8 45.0 %collective-permute-start.2 = (bf16[2,16,896]{2,1,0:T(8,128)(2,1)S(1)}, bf16[2,16,896]{2,1,0:T(8,128)(2,1)S(1)}, u32[]{:S(2)}, u32[]{:S(2)}) collective-permute-start(bf16[2,16,896]{2,1,0:T(8,128)(2,1)S(1)} %maximum_select_fusion.6), channel_id=1, source_target_pairs={{0,16},{8,24},{16,0},{24,8},{1,17},{9,25},{17,1},{25,9},{2,18},{10... | collective-permute-start | bytes 172040 | tf_op jit(solution)/shard_map/ppermute | solution.py:38
  60.8 4.9 %collective-permute-start.3 = (bf16[4,1,16,896]{3,2,0,1:T(8,128)(2,1)S(1)}, bf16[4,1,16,896]{3,2,0,1:T(8,128)(2,1)S(1)}, u32[]{:S(2)}, u32[]{:S(2)}) collective-permute-start(bf16[4,1,16,896]{3,2,0,1:T(8,128)(2,1)S(1)} %maximum_select_fusion.4), channel_id=1, source_target_pairs={{0,2},{2,0},{4,6},{6,4},{1,3},{3,1},{5,7},{7,5},{8,10},{10,8},{12,... | collective-permute-start | bytes 344072 | tf_op jit(solution)/shard_map/ppermute | solution.py:38
  65.7 6.6 %collective-permute-start.4 = (bf16[4,2,16,896]{3,2,0,1:T(8,128)(2,1)S(1)}, bf16[4,2,16,896]{3,2,0,1:T(8,128)(2,1)S(1)}, u32[]{:S(2)}, u32[]{:S(2)}) collective-permute-start(bf16[4,2,16,896]{3,2,0,1:T(8,128)(2,1)S(1)} %maximum_select_fusion.2), channel_id=1, source_target_pairs={{0,4},{2,6},{4,0},{6,2},{1,5},{3,7},{5,1},{7,3},{8,12},{10,14},{12... | collective-permute-start | bytes 688136 | tf_op jit(solution)/shard_map/ppermute | solution.py:38
  73.0 1.9 %collective-permute-start.5 = (bf16[16,14336]{1,0:T(8,128)(2,1)S(1)}, bf16[16,14336]{1,0:T(8,128)(2,1)S(1)}, u32[]{:S(2)}, u32[]{:S(2)}) collective-permute-start(bf16[16,14336]{1,0:T(8,128)(2,1)S(1)} %reshape.307), channel_id=1, source_target_pairs={{0,1},{1,0},{2,3},{3,2},{4,5},{5,4},{6,7},{7,6},{8,9},{9,8},{10,11... | collective-permute-start | bytes 1376264 | tf_op jit(solution)/shard_map/ppermute | solution.py:23
  75.5 3.8 %collective-permute-start.6 = (f32[1,64,32]{1,2,0:T(8,128)S(1)}, f32[1,64,32]{1,2,0:T(8,128)S(1)}, u32[]{:S(2)}, u32[]{:S(2)}) collective-permute-start(f32[1,64,32]{1,2,0:T(8,128)S(1)} %maximum_select_fusion.8), channel_id=1, source_target_pairs={{0,8},{8,0},{16,24},{24,16},{1,9},{9,1},{17,25},{25,17},{2,10},{10... | collective-permute-start | bytes 24584 | tf_op jit(solution)/shard_map/ppermute | solution.py:38
  79.3 4.8 %collective-permute-start.7 = (f32[2,64,32]{1,2,0:T(8,128)S(1)}, f32[2,64,32]{1,2,0:T(8,128)S(1)}, u32[]{:S(2)}, u32[]{:S(2)}) collective-permute-start(f32[2,64,32]{1,2,0:T(8,128)S(1)} %maximum_select_fusion.7), channel_id=1, source_target_pairs={{0,16},{8,24},{16,0},{24,8},{1,17},{9,25},{17,1},{25,9},{2,18},{10... | collective-permute-start | bytes 49160 | tf_op jit(solution)/shard_map/ppermute | solution.py:38
  84.1 4.3 %collective-permute-start.8 = (f32[4,1,64,32]{2,3,0,1:T(8,128)S(1)}, f32[4,1,64,32]{2,3,0,1:T(8,128)S(1)}, u32[]{:S(2)}, u32[]{:S(2)}) collective-permute-start(f32[4,1,64,32]{2,3,0,1:T(8,128)S(1)} %maximum_select_fusion.5), channel_id=1, source_target_pairs={{0,2},{2,0},{4,6},{6,4},{1,3},{3,1},{5,7},{7,5},{8,10},{10,8},{12,... | collective-permute-start | bytes 98312 | tf_op jit(solution)/shard_map/ppermute | solution.py:38
  88.5 5.0 %collective-permute-start.9 = (f32[4,2,64,32]{2,3,0,1:T(8,128)S(1)}, f32[4,2,64,32]{2,3,0,1:T(8,128)S(1)}, u32[]{:S(2)}, u32[]{:S(2)}) collective-permute-start(f32[4,2,64,32]{2,3,0,1:T(8,128)S(1)} %maximum_select_fusion.3), channel_id=1, source_target_pairs={{0,4},{2,6},{4,0},{6,2},{1,5},{3,7},{5,1},{7,3},{8,12},{10,14},{12... | collective-permute-start | bytes 196616 | tf_op jit(solution)/shard_map/ppermute | solution.py:38
  93.9 1.2 collective-permute-start.10
  104.3 1.4 collective-permute-start.11
  134.2 1.2 collective-permute-start.12
  144.7 1.4 collective-permute-start.13
  165.2 1.9 %collective-permute-start.14 = (bf16[16,14336]{1,0:T(8,128)(2,1)S(1)}, bf16[16,14336]{1,0:T(8,128)(2,1)S(1)}, u32[]{:S(2)}, u32[]{:S(2)}) collective-permute-start(bf16[16,14336]{1,0:T(8,128)(2,1)S(1)} %reshape.311), channel_id=1, source_target_pairs={{0,1},{1,0},{2,3},{3,2},{4,5},{5,4},{6,7},{7,6},{8,9},{9,8},{10,11... | collective-permute-start | bytes 1376264 | tf_op jit(solution)/shard_map/ppermute | solution.py:23

commit v3 on v1

--- a/solution.py
+++ b/solution.py
@@ -1,7 +1,10 @@
 import jax
 import jax.numpy as jnp
 from jax import lax
+from jax.experimental import pallas as pl
+from jax.experimental.pallas import tpu as pltpu
 from jax.sharding import Mesh, PartitionSpec as P
+
 
 ITERS = 2
 HIGHEST = lax.Precision.HIGHEST
@@ -27,6 +30,65 @@
     return lax.all_to_all(copies, axis, 0, 0, tiled=True)
 
 
+def exchanged(values, axis, dim):
+    position = lax.axis_index(axis)
+    size = lax.axis_size(axis)
+    pieces = [values]
+    for offset in range(1, size):
+        pairs = tuple((index, index ^ offset) for index in range(size))
+        pieces.append(lax.ppermute(values, axis, pairs))
+    bit = 1
+    while bit < size:
+        swap = (position & bit) != 0
+        pieces = [jnp.where(swap, pieces[i ^ bit], pieces[i]) for i in range(size)]
+        bit *= 2
+    return jnp.stack(pieces, axis=dim)
+
+
+def inverse_factor_kernel(own_ref, other_ref, inverse_ref, columns):
+    rank = own_ref.shape[0]
+    blocks = rank // 8
+    gram = own_ref[...] + other_ref[...]
+    for j in range(rank):
+        column = jnp.broadcast_to(gram[:, j : j + 1], (rank, 128))
+        for i in range(j // 8, blocks):
+            columns[j, i] = column[8 * i : 8 * i + 8]
+    row = lax.broadcasted_iota(jnp.int32, (8, 128), 0)
+    lane = lax.broadcasted_iota(jnp.int32, (8, 128), 1)
+    solved = [(lane == row + 8 * i).astype(jnp.float32) for i in range(blocks)]
+    for k in range(rank):
+        top, at = k // 8, k % 8
+        pivot = columns[k, top][at : at + 1]
+        scale = lax.rsqrt(pivot)
+        scale = scale * (1.5 - 0.5 * pivot * scale * scale)
+        lower = {i: columns[k, i] * scale for i in range(top, blocks)}
+        lower[top] = jnp.where(row > at, lower[top], 0.0)
+        solved_row = solved[top][at : at + 1] * scale
+        for i in range(top, blocks):
+            reduced = solved[i] - lower[i] * solved_row
+            solved[i] = jnp.where(row == at, solved_row, reduced) if i == top else reduced
+        for j in range(k + 1, rank):
+            entry = lower[j // 8][j % 8 : j % 8 + 1]
+            for i in range(j // 8, blocks):
+                columns[j, i] = columns[j, i] - lower[i] * entry
+    for i in range(blocks):
+        inverse_ref[8 * i : 8 * i + 8, :] = solved[i][:, :rank]
+
+
+def inverse_factor(own_gram, other_gram):
+    rank = own_gram.shape[0]
+    return pl.pallas_call(
+        inverse_factor_kernel,
+        out_shape=jax.ShapeDtypeStruct((rank, rank), jnp.float32),
+        in_specs=[pl.BlockSpec(memory_space=pltpu.VMEM)] * 2,
+        out_specs=pl.BlockSpec(memory_space=pltpu.VMEM),
+        scratch_shapes=[pltpu.VMEM((rank, rank // 8, 8, 128), jnp.float32)],
+        compiler_params=pltpu.CompilerParams(vmem_limit_bytes=4 * 1024 * 1024),
+        cost_estimate=pl.CostEstimate(flops=4000000, bytes_accessed=12288, transcendentals=rank),
+        name="inverse_factor",
+    )(own_gram, other_gram)
+
+
 def gather_chips(values):
     by_hi = spread(values, "hi")
     return spread(by_hi, "lo").swapaxes(0, 1)
@@ -41,11 +103,7 @@
 
 def orthonormal_basis(p_rows, p_own):
     own_gram = jnp.dot(p_rows.T, p_rows, precision=HIGHEST)
-    gram_matrix = own_gram + swap_cores(own_gram)
-    factor = jnp.linalg.cholesky(gram_matrix)
-    inverse = lax.linalg.triangular_solve(
-        factor, jnp.eye(factor.shape[0], dtype=jnp.float32), left_side=True, lower=True
-    )
+    inverse = inverse_factor(own_gram, swap_cores(own_gram))
     basis = lax.dot_general(p_rows, inverse, (((1,), (1,)), ((), ())), precision=HIGHEST)
     basis_own = lax.dot_general(p_own, inverse, (((1,), (1,)), ((), ())), precision=HIGHEST)
     return basis, basis_own
@@ -63,26 +121,29 @@
     blocks = own_rows.reshape(rows, chips, width).transpose(1, 0, 2)
     block = lax.all_to_all(blocks, CHIP, 0, 0, tiled=True).reshape(chips * rows, width)
 
-    kept = lax.dynamic_slice_in_dim(q_start, core * half, half, 0)
-    given = lax.dynamic_slice_in_dim(q_start, (1 - core) * half, half, 0)
-    taken = swap_cores(given)
-    first = jnp.where(core == 0, kept, taken)
-    second = jnp.where(core == 0, taken, kept)
-    own, other = gather_right(jnp.concatenate([first, second], axis=1))
-    p_mine = product_transposed(own_rows, own)
-    p_theirs = product_transposed(own_rows, other)
-    p_own = jnp.where(
-        core == 0,
-        jnp.concatenate([p_mine, p_theirs], axis=1),
-        jnp.concatenate([p_theirs, p_mine], axis=1),
+    shift = width - 2 * shard_cols + shard_cols % 128
+    placed = jnp.where(
+        core == 0, jnp.pad(q_start, ((0, 0), (0, shift))), jnp.pad(q_start, ((0, 0), (shift, 0)))
     )
+    by_hi = exchanged(placed, "hi", 0)
+    own = exchanged(by_hi, "lo", 1)
+    other = swap_cores(own)
+    rest = width - shard_cols - shift
+    even = jnp.pad(jnp.where(core == 0, own, other), ((0, 0), (0, 0), (0, 0), (0, rest)))
+    odd = jnp.pad(jnp.where(core == 0, other, own), ((0, 0), (0, 0), (0, 0), (rest, 0)))
+    start = (even + odd).transpose(2, 0, 1, 3).reshape(rank, cols)
+    p_own = product_transposed(own_rows, start)
     for iteration in range(ITERS):
         if iteration > 0:
             term = product_transposed(block, right_factor).reshape(chips, rows, rank)
             p_own = jnp.sum(lax.all_to_all(term, CHIP, 0, 0, tiled=True), axis=0)
         if replicas > 1:
             p_own = lax.psum(p_own, "rep")
-        p_rows = spread(p_own, CHIP).reshape(chips * rows, rank)
+        if iteration > 0:
+            p_rows = spread(p_own, CHIP).reshape(chips * rows, rank)
+        else:
+            by_lo = exchanged(p_own, "lo", 0)
+            p_rows = exchanged(by_lo, "hi", 0).reshape(chips * rows, rank)
         basis, basis_own = orthonormal_basis(p_rows, p_own)
         q_term = transposed_product(basis.astype(jnp.bfloat16), block)
         q_chip = q_term + swap_cores(q_term)

time: 155 us -> 126 us (0.81)
  blocking collectives: 67.5 us -> 42.5 us
  starting transfers between devices: 9.23 us -> 25.3 us
  other arithmetic: 17.1 us -> 3.42 us
  waiting for transfers between devices: 40.2 us -> 34.5 us
  matrix products: 11.4 us -> 7.67 us
    ppermute x0 -> x12, waiting for transfers between devices: none -> 28.4 us  [exchanged(): pieces.append(lax.ppermute(values, axis, pairs))]
    all_to_all x1, waiting for transfers between devices: 27.7 us -> 0.01 us  [on_device(): lax.all_to_all(blocks, CHIP, 0, 0, tiled=True).reshape(chips * rows, width)]
    all_to_all x5 -> x3, blocking collectives: 51.5 us -> 29.1 us  [spread(): return lax.all_to_all(copies, axis, 0, 0, tiled=True)]
    ppermute x0 -> x12, starting transfers between devices: none -> 17.5 us  [exchanged(): pieces.append(lax.ppermute(values, axis, pairs))]
    another operation x10, other arithmetic: 13.4 us -> 0.36 us  [exchanged(): return jnp.stack(pieces, axis=dim)]
    all_to_all x1 -> x0, waiting for transfers between devices: 5.9 us -> none  [spread(): return lax.all_to_all(copies, axis, 0, 0, tiled=True)]
    all_to_all x1 -> x0, starting transfers between devices: 3.73 us -> none  [spread(): return lax.all_to_all(copies, axis, 0, 0, tiled=True)]
    dot_general x2, matrix products: 3.81 us -> 0.81 us  [transposed_product(): lax.dot_general(left, right, (((0,), (0,)), ((), ())), preferred_element_...]
  transfers between devices with their start and end apart: 9 -> 19, of which waited for: 9 -> 13; matrix products, arithmetic and copies ran while one was open for 9% -> 9% of each run, Pallas kernels for 0% -> 0%
where the time goes in v3:
time: 126 us; the launch traced here: 125 us
  blocking collectives  42.5 us (34%)
  waiting for transfers between devices  34.5 us (27%)
  starting transfers between devices  25.3 us (20%)
  local copies, waits for them, and re-layouts  9.33 us (7%)
  matrix products  7.67 us (6%)
  other arithmetic  3.42 us (3%)
    all_to_all x3, blocking collectives, spread(): return lax.all_to_all(copies, axis, 0, 0, tiled=True)  29.1 us
    ppermute x12, waiting for transfers between devices, exchanged(): pieces.append(lax.ppermute(values, axis, pairs))  28.4 us
    ppermute x12, starting transfers between devices, exchanged(): pieces.append(lax.ppermute(values, axis, pairs))  17.5 us
    all_to_all x1, blocking collectives, on_device(): p_own = jnp.sum(lax.all_to_all(term, CHIP, 0, 0, tiled=True), axis=0)  13.4 us
    all_to_all x1, starting transfers between devices, on_device(): lax.all_to_all(blocks, CHIP, 0, 0, tiled=True).reshape(chips * rows, width)  7.14 us
    ppermute x6, waiting for transfers between devices, swap_cores(): return lax.ppermute(values, 'core', SWAP)  6.15 us
    dot_general x2, matrix products, product_transposed(): lax.dot_general(left, right, (((1,), (1,)), ((), ())), preferred_element_...  3.01 us
  transfers between devices with their start and end apart: 19, of which 13 were waited for; matrix products, arithmetic and copies ran while one was open for 9% of the time, Pallas kernels for 0%

profile of v3, /device:TPU:0, one launch (start us, length us, event | category | flops | bytes accessed | tf_op | source)
XLA Modules:
  0.0 125.0 jit_solution(6110560118500080501)
XLA Ops:
  0.6 0.9 pad_select_fusion
  1.6 5.1 %collective-permute-start = (bf16[32,512]{1,0:T(8,128)(2,1)S(1)}, bf16[32,512]{1,0:T(8,128)(2,1)S(1)}, u32[]{:S(2)}, u32[]{:S(2)}) collective-permute-start(bf16[32,512]{1,0:T(8,128)(2,1)S(1)} %pad_select_fusion), channel_id=1, source_target_pairs={{0,24},{8,16},{16,8},{24,0},{1,25},{9,17},{17,9},{25,1},{2,26},{10... | collective-permute-start | bytes 98312 | tf_op jit(solution)/shard_map/ppermute | solution.py:39
  6.7 0.6 collective-permute-start.2
  7.3 1.7 %copy.20 = bf16[8,8,16,896]{3,2,1,0:T(8,128)(2,1)S(1)} copy(bf16[8,8,16,896]{3,1,2,0:T(8,128)(2,1)} %bitcast.90) | data formatting | bytes 3670016
  9.1 1.6 %copy.14 = bf16[16,64,896]{2,1,0:T(8,128)(2,1)} copy(bf16[16,64,896]{2,0,1:T(8,128)(2,1)S(1)} %bitcast.91) | data formatting | bytes 3670016 | tf_op jit(solution)/shard_map/transpose | solution.py:121
  10.7 7.1 %all-to-all-start = ((bf16[16,64,896]{2,1,0:T(8,128)(2,1)}), bf16[16,64,896]{2,1,0:T(8,128)(2,1)S(1)}, u32[]{:S(2)}, u32[]{:S(2)}) async-start(bf16[16,64,896]{2,1,0:T(8,128)(2,1)} %copy.14), calls=%async_computation | async-start | bytes 3670016 | tf_op jit(solution)/shard_map/all_to_all | solution.py:122
  17.9 0.1 select_bitcast_fusion.11
  18.1 2.9 %collective-permute-start.3 = (bf16[4,32,512]{2,1,0:T(8,128)(2,1)S(1)}, bf16[4,32,512]{2,1,0:T(8,128)(2,1)S(1)}, u32[]{:S(2)}, u32[]{:S(2)}) collective-permute-start(bf16[4,32,512]{2,1,0:T(8,128)(2,1)S(1)} %pad_maximum_fusion.2), channel_id=1, source_target_pairs={{0,6},{2,4},{4,2},{6,0},{1,7},{3,5},{5,3},{7,1},{8,14},{10,12},{12... | collective-permute-start | bytes 393224 | tf_op jit(solution)/shard_map/ppermute | solution.py:39
  21.0 0.6 collective-permute-start.4
  21.5 0.1 collective-permute-start.5
  21.6 9.3 %collective-permute-done.3 = bf16[4,32,512]{2,1,0:T(8,128)(2,1)S(1)} collective-permute-done((bf16[4,32,512]{2,1,0:T(8,128)(2,1)S(1)}, bf16[4,32,512]{2,1,0:T(8,128)(2,1)S(1)}, u32[]{:S(2)}, u32[]{:S(2)}) %collective-permute-start.3) | collective-permute-done | bytes 131104 | tf_op jit(solution)/shard_map/ppermute | solution.py:39
  30.9 6.8 %collective-permute-done.4 = bf16[4,32,512]{2,1,0:T(8,128)(2,1)S(1)} collective-permute-done((bf16[4,32,512]{2,1,0:T(8,128)(2,1)S(1)}, bf16[4,32,512]{2,1,0:T(8,128)(2,1)S(1)}, u32[]{:S(2)}, u32[]{:S(2)}) %collective-permute-start.4) | collective-permute-done | bytes 131104 | tf_op jit(solution)/shard_map/ppermute | solution.py:39
  37.9 1.9 %collective-permute-done.6 = bf16[4,4,32,512]{3,2,0,1:T(8,128)(2,1)S(1)} collective-permute-done((bf16[4,4,32,512]{3,2,0,1:T(8,128)(2,1)S(1)}, bf16[4,4,32,512]{3,2,0,1:T(8,128)(2,1)S(1)}, u32[]{:S(2)}, u32[]{:S(2)}) %collective-permute-start.6) | collective-permute-done | bytes 524320 | tf_op jit(solution)/shard_map/ppermute | solution.py:25
  39.9 0.1 add_bitcast_fusion
  40.1 0.7 copy.12
  40.8 1.6 %reshape.27 = bf16[32,14336]{1,0:T(8,128)(2,1)} reshape(bf16[32,4,4,896]{3,2,1,0:T(4,128)(2,1)S(1)} %copy.12) | data formatting | bytes 1835008 | tf_op jit(solution)/shard_map/reshape | solution.py:134
  42.4 2.4 %fusion.4 = f32[64,32]{0,1:T(8,128)S(1)} fusion(bf16[32,14336]{1,0:T(8,128)(2,1)} %reshape.27, bf16[1,64,14336]{2,1,0:T(8,128)(2,1)} %param.2), kind=kOutput, calls=%fused_computation.8 | convolution fusion | flops 58720256 | bytes 2760704 | tf_op jit(solution)/shard_map/dot_general | solution.py:21
  44.8 1.0 collective-permute-start.7
  45.8 2.6 %collective-permute-start.8 = (f32[64,32]{0,1:T(8,128)S(1)}, f32[64,32]{0,1:T(8,128)S(1)}, u32[]{:S(2)}, u32[]{:S(2)}) collective-permute-start(f32[64,32]{0,1:T(8,128)S(1)} %fusion.4), channel_id=1, source_target_pairs={{0,4},{2,6},{4,0},{6,2},{1,5},{3,7},{5,1},{7,3},{8,12},{10,14},{12... | collective-permute-start | bytes 24584 | tf_op jit(solution)/shard_map/ppermute | solution.py:39
  48.4 1.2 collective-permute-done.7
  49.7 1.7 %collective-permute-done.8 = f32[64,32]{0,1:T(8,128)S(1)} collective-permute-done((f32[64,32]{0,1:T(8,128)S(1)}, f32[64,32]{0,1:T(8,128)S(1)}, u32[]{:S(2)}, u32[]{:S(2)}) %collective-permute-start.8) | collective-permute-done | bytes 8224 | tf_op jit(solution)/shard_map/ppermute | solution.py:39
  51.4 3.5 %collective-permute-done.9 = f32[64,32]{0,1:T(8,128)S(1)} collective-permute-done((f32[64,32]{0,1:T(8,128)S(1)}, f32[64,32]{0,1:T(8,128)S(1)}, u32[]{:S(2)}, u32[]{:S(2)}) %collective-permute-start.9) | collective-permute-done | bytes 8224 | tf_op jit(solution)/shard_map/ppermute | solution.py:39
  54.9 2.4 %collective-permute-start.10 = (f32[4,64,32]{1,2,0:T(8,128)S(1)}, f32[4,64,32]{1,2,0:T(8,128)S(1)}, u32[]{:S(2)}, u32[]{:S(2)}) collective-permute-start(f32[4,64,32]{1,2,0:T(8,128)S(1)} %pad_maximum_fusion.3), channel_id=1, source_target_pairs={{0,24},{8,16},{16,8},{24,0},{1,25},{9,17},{17,9},{25,1},{2,26},{10... | collective-permute-start | bytes 98312 | tf_op jit(solution)/shard_map/ppermute | solution.py:39
  57.3 2.1 %collective-permute-start.12 = (f32[4,64,32]{1,2,0:T(8,128)S(1)}, f32[4,64,32]{1,2,0:T(8,128)S(1)}, u32[]{:S(2)}, u32[]{:S(2)}) collective-permute-start(f32[4,64,32]{1,2,0:T(8,128)S(1)} %pad_maximum_fusion.3), channel_id=1, source_target_pairs={{0,8},{8,0},{16,24},{24,16},{1,9},{9,1},{17,25},{25,17},{2,10},{10... | collective-permute-start | bytes 98312 | tf_op jit(solution)/shard_map/ppermute | solution.py:39
  59.4 2.2 %collective-permute-done.10 = f32[4,64,32]{1,2,0:T(8,128)S(1)} collective-permute-done((f32[4,64,32]{1,2,0:T(8,128)S(1)}, f32[4,64,32]{1,2,0:T(8,128)S(1)}, u32[]{:S(2)}, u32[]{:S(2)}) %collective-permute-start.10) | collective-permute-done | bytes 32800 | tf_op jit(solution)/shard_map/ppermute | solution.py:39
  61.6 3.6 %collective-permute-done.11 = f32[4,64,32]{1,2,0:T(8,128)S(1)} collective-permute-done((f32[4,64,32]{1,2,0:T(8,128)S(1)}, f32[4,64,32]{1,2,0:T(8,128)S(1)}, u32[]{:S(2)}, u32[]{:S(2)}) %collective-permute-start.11) | collective-permute-done | bytes 32800 | tf_op jit(solution)/shard_map/ppermute | solution.py:39
  65.3 0.4 convolution_bitcast_fusion.2.own_ref
  65.8 0.2 copy.13
  65.9 0.2 reshape.28
  66.2 0.7 collective-permute-done.13.other_ref
  66.9 0.6 inverse_factor.2
  67.5 0.3 convolution_convert_fusion.1
  67.8 0.4 fusion.16
  68.2 0.2 collective-permute-start.14
  68.4 1.2 collective-permute-done.14
  69.6 0.6 convolution_bitcast_fusion
  70.2 0.1 reshape.30
  70.4 0.2 reshape.35
  70.6 13.4 %all_to_all.25 = f32[16,1,2048]{2,1,0:T(1,128)S(1)} all-to-all(f32[16,1,2048]{2,1,0:T(1,128)S(1)} %reshape.35), channel_id=1, replica_groups=mesh['rep'=1,'hi'=4,'lo'=4,'core'=2] {'hi','lo'}, dimensions={0} | all-to-all | bytes 262144 | tf_op jit(solution)/shard_map/all_to_all | solution.py:139
  84.0 0.5 broadcast.12
  84.5 0.9 reduce
  85.5 0.1 reshape.36
  85.7 0.2 reshape.37
  85.8 10.7 %all_to_all.26 = f32[16,1,2048]{2,1,0:T(1,128)S(1)} all-to-all(f32[16,1,2048]{2,1,0:T(1,128)S(1)} %reshape.37), channel_id=1, replica_groups=mesh['rep'=1,'hi'=4,'lo'=4,'core'=2] {'hi','lo'}, dimensions={0} | all-to-all | bytes 262144 | tf_op jit(solution)/shard_map/all_to_all | solution.py:30
  96.6 0.9 reduce.1
  97.5 0.1 reshape.38
  97.6 0.4 convolution_bitcast_fusion.1.own_ref
  98.1 0.2 copy.16
  98.2 0.1 reshape.31
  98.4 0.9 collective-permute-done.15.other_ref
  99.3 0.6 inverse_factor.3
  99.9 0.3 convolution_convert_fusion
  100.1 0.4 fusion.17
  100.5 0.2 collective-permute-start.16
  100.8 1.2 collective-permute-done.16
  102.0 8.6 %all_to_all.27 = bf16[4,16,896]{2,1,0:T(8,128)(2,1)S(1)} all-to-all(bf16[4,16,896]{2,1,0:T(8,128)(2,1)S(1)} %broadcast_in_dim.9), channel_id=1, replica_groups=mesh['rep'=1,'hi'=4,'lo'=4,'core'=2] {'hi'}, dimensions={0} | all-to-all | bytes 229376 | tf_op jit(solution)/shard_map/all_to_all | solution.py:30
  110.6 0.1 broadcast_in_dim.10
  110.8 9.7 %all_to_all.28 = bf16[4,4,16,896]{3,1,2,0:T(4,128)(2,1)S(1)} all-to-all(bf16[4,4,16,896]{3,1,2,0:T(4,128)(2,1)S(1)} %broadcast_in_dim.10), channel_id=1, replica_groups=mesh['rep'=1,'hi'=4,'lo'=4,'core'=2] {'lo'}, dimensions={0} | all-to-all | bytes 917504 | tf_op jit(solution)/shard_map/all_to_all | solution.py:30
  120.5 0.4 copy.18
  120.9 0.3 reshape.32
  121.3 0.8 fusion.14
  122.0 0.7 constant_dynamic-slice_fusion
  122.8 0.3 collective-permute-done.17
  123.1 1.9 %fusion.1 = bf16[1,64,14336]{2,1,0:T(8,128)(2,1)} fusion(bf16[1,64,14336]{2,1,0:T(8,128)(2,1)S(1)} %copy-done, bf16[16,14336]{1,0:T(8,128)(2,1)S(1)} %collective-permute-done.17, bf16[16,14336]{1,0:T(8,128)(2,1)S(1)} %reshape.32, bf16[64,16]{0,1:T(8,128)(2,1)S(1)} %get-tuple-element.20, bf16[64,16]{0,1:T(8,128)(2,1)S(1)} %get-tuple-element.19), kind=kOutput, calls=%fused_computation.2 | convolution fusion | flops 63315968 | bytes 4591616 | tf_op jit(solution)/shard_map/dot_general | solution.py:159
  (35 shorter events, 0.9 us)
Async XLA Ops:
  1.6 16.3 %collective-permute-start = (bf16[32,512]{1,0:T(8,128)(2,1)S(1)}, bf16[32,512]{1,0:T(8,128)(2,1)S(1)}, u32[]{:S(2)}, u32[]{:S(2)}) collective-permute-start(bf16[32,512]{1,0:T(8,128)(2,1)S(1)} %pad_select_fusion), channel_id=1, source_target_pairs={{0,24},{8,16},{16,8},{24,0},{1,25},{9,17},{17,9},{25,1},{2,26},{10... | collective-permute-start | bytes 98312 | tf_op jit(solution)/shard_map/ppermute | solution.py:39
  6.7 11.2 %collective-permute-start.1 = (bf16[32,512]{1,0:T(8,128)(2,1)S(1)}, bf16[32,512]{1,0:T(8,128)(2,1)S(1)}, u32[]{:S(2)}, u32[]{:S(2)}) collective-permute-start(bf16[32,512]{1,0:T(8,128)(2,1)S(1)} %pad_select_fusion), channel_id=1, source_target_pairs={{0,16},{8,24},{16,0},{24,8},{1,17},{9,25},{17,1},{25,9},{2,18},{10... | collective-permute-start | bytes 98312 | tf_op jit(solution)/shard_map/ppermute | solution.py:39
  6.7 11.2 %collective-permute-start.2 = (bf16[32,512]{1,0:T(8,128)(2,1)S(1)}, bf16[32,512]{1,0:T(8,128)(2,1)S(1)}, u32[]{:S(2)}, u32[]{:S(2)}) collective-permute-start(bf16[32,512]{1,0:T(8,128)(2,1)S(1)} %pad_select_fusion), channel_id=1, source_target_pairs={{0,8},{8,0},{16,24},{24,16},{1,9},{9,1},{17,25},{25,17},{2,10},{10... | collective-permute-start | bytes 98312 | tf_op jit(solution)/shard_map/ppermute | solution.py:39
  10.7 7.2 %copy-start.1 = (bf16[32,448]{1,0:T(8,128)(2,1)S(1)}, bf16[32,448]{1,0:T(8,128)(2,1)}, u32[]{:S(2)}) copy-start(bf16[32,448]{1,0:T(8,128)(2,1)} %param.3) | copy-start | bytes 86020
  10.7 57.0 %all-to-all-start = ((bf16[16,64,896]{2,1,0:T(8,128)(2,1)}), bf16[16,64,896]{2,1,0:T(8,128)(2,1)S(1)}, u32[]{:S(2)}, u32[]{:S(2)}) async-start(bf16[16,64,896]{2,1,0:T(8,128)(2,1)} %copy.14), calls=%async_computation | async-start | bytes 3670016 | tf_op jit(solution)/shard_map/all_to_all | solution.py:122
  18.1 12.9 %collective-permute-start.3 = (bf16[4,32,512]{2,1,0:T(8,128)(2,1)S(1)}, bf16[4,32,512]{2,1,0:T(8,128)(2,1)S(1)}, u32[]{:S(2)}, u32[]{:S(2)}) collective-permute-start(bf16[4,32,512]{2,1,0:T(8,128)(2,1)S(1)} %pad_maximum_fusion.2), channel_id=1, source_target_pairs={{0,6},{2,4},{4,2},{6,0},{1,7},{3,5},{5,3},{7,1},{8,14},{10,12},{12... | collective-permute-start | bytes 393224 | tf_op jit(solution)/shard_map/ppermute | solution.py:39
  21.0 16.7 %collective-permute-start.4 = (bf16[4,32,512]{2,1,0:T(8,128)(2,1)S(1)}, bf16[4,32,512]{2,1,0:T(8,128)(2,1)S(1)}, u32[]{:S(2)}, u32[]{:S(2)}) collective-permute-start(bf16[4,32,512]{2,1,0:T(8,128)(2,1)S(1)} %pad_maximum_fusion.2), channel_id=1, source_target_pairs={{0,4},{2,6},{4,0},{6,2},{1,5},{3,7},{5,1},{7,3},{8,12},{10,14},{12... | collective-permute-start | bytes 393224 | tf_op jit(solution)/shard_map/ppermute | solution.py:39
  21.5 16.2 %collective-permute-start.5 = (bf16[4,32,512]{2,1,0:T(8,128)(2,1)S(1)}, bf16[4,32,512]{2,1,0:T(8,128)(2,1)S(1)}, u32[]{:S(2)}, u32[]{:S(2)}) collective-permute-start(bf16[4,32,512]{2,1,0:T(8,128)(2,1)S(1)} %pad_maximum_fusion.2), channel_id=1, source_target_pairs={{0,2},{2,0},{4,6},{6,4},{1,3},{3,1},{5,7},{7,5},{8,10},{10,8},{12,... | collective-permute-start | bytes 393224 | tf_op jit(solution)/shard_map/ppermute | solution.py:39
  37.9 2.0 %collective-permute-start.6 = (bf16[4,4,32,512]{3,2,0,1:T(8,128)(2,1)S(1)}, bf16[4,4,32,512]{3,2,0,1:T(8,128)(2,1)S(1)}, u32[]{:S(2)}, u32[]{:S(2)}) collective-permute-start(bf16[4,4,32,512]{3,2,0,1:T(8,128)(2,1)S(1)} %pad_maximum_fusion), channel_id=1, source_target_pairs={{0,1},{1,0},{2,3},{3,2},{4,5},{5,4},{6,7},{7,6},{8,9},{9,8},{10,11... | collective-permute-start | bytes 1572872 | tf_op jit(solution)/shard_map/ppermute | solution.py:25
  44.8 4.9 %collective-permute-start.7 = (f32[64,32]{0,1:T(8,128)S(1)}, f32[64,32]{0,1:T(8,128)S(1)}, u32[]{:S(2)}, u32[]{:S(2)}) collective-permute-start(f32[64,32]{0,1:T(8,128)S(1)} %fusion.4), channel_id=1, source_target_pairs={{0,6},{2,4},{4,2},{6,0},{1,7},{3,5},{5,3},{7,1},{8,14},{10,12},{12... | collective-permute-start | bytes 24584 | tf_op jit(solution)/shard_map/ppermute | solution.py:39
  45.8 5.6 %collective-permute-start.8 = (f32[64,32]{0,1:T(8,128)S(1)}, f32[64,32]{0,1:T(8,128)S(1)}, u32[]{:S(2)}, u32[]{:S(2)}) collective-permute-start(f32[64,32]{0,1:T(8,128)S(1)} %fusion.4), channel_id=1, source_target_pairs={{0,4},{2,6},{4,0},{6,2},{1,5},{3,7},{5,1},{7,3},{8,12},{10,14},{12... | collective-permute-start | bytes 24584 | tf_op jit(solution)/shard_map/ppermute | solution.py:39
  48.4 6.5 %collective-permute-start.9 = (f32[64,32]{0,1:T(8,128)S(1)}, f32[64,32]{0,1:T(8,128)S(1)}, u32[]{:S(2)}, u32[]{:S(2)}) collective-permute-start(f32[64,32]{0,1:T(8,128)S(1)} %fusion.4), channel_id=1, source_target_pairs={{0,2},{2,0},{4,6},{6,4},{1,3},{3,1},{5,7},{7,5},{8,10},{10,8},{12,... | collective-permute-start | bytes 24584 | tf_op jit(solution)/shard_map/ppermute | solution.py:39
  54.9 6.7 %collective-permute-start.10 = (f32[4,64,32]{1,2,0:T(8,128)S(1)}, f32[4,64,32]{1,2,0:T(8,128)S(1)}, u32[]{:S(2)}, u32[]{:S(2)}) collective-permute-start(f32[4,64,32]{1,2,0:T(8,128)S(1)} %pad_maximum_fusion.3), channel_id=1, source_target_pairs={{0,24},{8,16},{16,8},{24,0},{1,25},{9,17},{17,9},{25,1},{2,26},{10... | collective-permute-start | bytes 98312 | tf_op jit(solution)/shard_map/ppermute | solution.py:39
  57.3 7.9 %collective-permute-start.11 = (f32[4,64,32]{1,2,0:T(8,128)S(1)}, f32[4,64,32]{1,2,0:T(8,128)S(1)}, u32[]{:S(2)}, u32[]{:S(2)}) collective-permute-start(f32[4,64,32]{1,2,0:T(8,128)S(1)} %pad_maximum_fusion.3), channel_id=1, source_target_pairs={{0,16},{8,24},{16,0},{24,8},{1,17},{9,25},{17,1},{25,9},{2,18},{10... | collective-permute-start | bytes 98312 | tf_op jit(solution)/shard_map/ppermute | solution.py:39
  57.3 7.9 %collective-permute-start.12 = (f32[4,64,32]{1,2,0:T(8,128)S(1)}, f32[4,64,32]{1,2,0:T(8,128)S(1)}, u32[]{:S(2)}, u32[]{:S(2)}) collective-permute-start(f32[4,64,32]{1,2,0:T(8,128)S(1)} %pad_maximum_fusion.3), channel_id=1, source_target_pairs={{0,8},{8,0},{16,24},{24,16},{1,9},{9,1},{17,25},{25,17},{2,10},{10... | collective-permute-start | bytes 98312 | tf_op jit(solution)/shard_map/ppermute | solution.py:39
  65.7 1.2 collective-permute-start.13
  68.2 1.4 %collective-permute-start.14 = (f32[32,896]{1,0:T(8,128)S(1)}, f32[32,896]{1,0:T(8,128)S(1)}, u32[]{:S(2)}, u32[]{:S(2)}) collective-permute-start(f32[32,896]{1,0:T(8,128)S(1)} %fusion.16), channel_id=1, source_target_pairs={{0,1},{1,0},{2,3},{3,2},{4,5},{5,4},{6,7},{7,6},{8,9},{9,8},{10,11... | collective-permute-start | bytes 344072 | tf_op jit(solution)/shard_map/ppermute | solution.py:25
  98.0 1.2 collective-permute-start.15
  100.5 1.4 %collective-permute-start.16 = (f32[32,896]{1,0:T(8,128)S(1)}, f32[32,896]{1,0:T(8,128)S(1)}, u32[]{:S(2)}, u32[]{:S(2)}) collective-permute-start(f32[32,896]{1,0:T(8,128)S(1)} %fusion.17), channel_id=1, source_target_pairs={{0,1},{1,0},{2,3},{3,2},{4,5},{5,4},{6,7},{7,6},{8,9},{9,8},{10,11... | collective-permute-start | bytes 344072 | tf_op jit(solution)/shard_map/ppermute | solution.py:25
  110.6 12.5 %copy-start = (bf16[1,64,14336]{2,1,0:T(8,128)(2,1)S(1)}, bf16[1,64,14336]{2,1,0:T(8,128)(2,1)}, u32[]{:S(2)}) copy-start(bf16[1,64,14336]{2,1,0:T(8,128)(2,1)} %param.2) | copy-start | bytes 5505028
  121.2 1.9 %collective-permute-start.17 = (bf16[16,14336]{1,0:T(8,128)(2,1)S(1)}, bf16[16,14336]{1,0:T(8,128)(2,1)S(1)}, u32[]{:S(2)}, u32[]{:S(2)}) collective-permute-start(bf16[16,14336]{1,0:T(8,128)(2,1)S(1)} %reshape.32), channel_id=1, source_target_pairs={{0,1},{1,0},{2,3},{3,2},{4,5},{5,4},{6,7},{7,6},{8,9},{9,8},{10,11... | collective-permute-start | bytes 1376264 | tf_op jit(solution)/shard_map/ppermute | solution.py:25

commit v4 on v3

v4 whole, which is shorter than its diff:
```python
import jax
import jax.numpy as jnp
from jax import lax
from jax.experimental import pallas as pl
from jax.experimental.pallas import tpu as pltpu
from jax.sharding import Mesh, PartitionSpec as P


ITERS = 2
HIGHEST = lax.Precision.HIGHEST
CHIP = ("hi", "lo")
ROWS = ("hi", "lo", "core")
SWAP = ((0, 1), (1, 0))


def swap_cores(values):
    return lax.ppermute(values, "core", SWAP)


def spread(values, axis):
    copies = jnp.broadcast_to(values[None], (lax.axis_size(axis),) + values.shape)
    return lax.all_to_all(copies, axis, 0, 0, tiled=True)


def exchanged(values, axis, dim):
    position = lax.axis_index(axis)
    size = lax.axis_size(axis)
    pieces = [values]
    for offset in range(1, size):
        pairs = tuple((index, index ^ offset) for index in range(size))
        pieces.append(lax.ppermute(values, axis, pairs))
    bit = 1
    while bit < size:
        swap = (position & bit) != 0
        pieces = [jnp.where(swap, pieces[i ^ bit], pieces[i]) for i in range(size)]
        bit *= 2
    return jnp.stack(pieces, axis=dim)


def kernel_call(kernel, out_shape, flops, scratch=()):
    single = not isinstance(out_shape, tuple)
    outs = (out_shape,) if single else out_shape
    vmem = pl.BlockSpec(memory_space=pltpu.VMEM)
    return lambda *args: pl.pallas_call(
        kernel,
        out_shape=out_shape,
        in_specs=[vmem] * len(args),
        out_specs=vmem if single else (vmem,) * len(outs),
        scratch_shapes=list(scratch),
        compiler_params=pltpu.CompilerParams(vmem_limit_bytes=16 * 1024 * 1024),
        cost_estimate=pl.CostEstimate(
            flops=flops, bytes_accessed=sum(a.size * a.dtype.itemsize for a in args), transcendentals=0
        ),
    )(*args)


def packed_rows(wide, groups):
    per = wide.shape[0] // groups
    return jnp.concatenate([wide[per * g : per * g + per, :] for g in range(groups)], axis=1)


def cut_kernel(rows_ref, blocks_ref, held, read_semaphores, write_semaphores):
    chips, _, width = blocks_ref.shape
    reads = [
        pltpu.make_async_copy(
            rows_ref.at[:, width * chip : width * chip + width], held.at[chip], read_semaphores.at[chip]
        )
        for chip in range(chips)
    ]
    writes = [
        pltpu.make_async_copy(held.at[chip], blocks_ref.at[chip], write_semaphores.at[chip])
        for chip in range(chips)
    ]
    for read in reads:
        read.start()
    for read, write in zip(reads, writes):
        read.wait()
        write.start()
    for write in writes:
        write.wait()


def cut(own_rows, chips):
    rows, cols = own_rows.shape
    width = cols // chips
    if width % 128:
        return own_rows.reshape(rows, chips, width).transpose(1, 0, 2)
    return pl.pallas_call(
        cut_kernel,
        out_shape=jax.ShapeDtypeStruct((chips, rows, width), own_rows.dtype),
        in_specs=[pl.BlockSpec(memory_space=pltpu.HBM)],
        out_specs=pl.BlockSpec(memory_space=pltpu.HBM),
        scratch_shapes=[
            pltpu.VMEM((chips, rows, width), own_rows.dtype),
            pltpu.SemaphoreType.DMA((chips,)),
            pltpu.SemaphoreType.DMA((chips,)),
        ],
        compiler_params=pltpu.CompilerParams(vmem_limit_bytes=66_000_000),
        cost_estimate=pl.CostEstimate(flops=1000, bytes_accessed=4 * rows * cols, transcendentals=0),
        name="cut",
    )(own_rows)


def first_p_kernel(own_ref, other_ref, blocks_ref, p_ref):
    chips, rows, width = blocks_ref.shape
    _, lo, rank, placed = own_ref.shape
    rest = width - placed
    is_even = lax.axis_index("core") == 0
    total = jnp.zeros((rows, rank), jnp.float32)
    for chip in range(chips):
        own, other = own_ref[chip // lo, chip % lo], other_ref[chip // lo, chip % lo]
        even = jnp.where(is_even, own, other)
        odd = jnp.where(is_even, other, own)
        for part, start in ((even, 0), (odd, rest)):
            total += lax.dot_general(
                blocks_ref[chip, :, start : start + placed],
                part,
                (((1,), (1,)), ((), ())),
                preferred_element_type=jnp.float32,
            )
    p_ref[...] = packed_rows(total, 128 // rank)


def next_p_kernel(q_ref, block_ref, p_ref):
    chips, rows, width = block_ref.shape
    rank = q_ref.shape[0]
    groups = 128 // rank
    per = rows // groups
    right = q_ref[...]
    parts = [
        lax.dot_general(
            block_ref[:, per * g : per * g + per, :].reshape(chips * per, width),
            right,
            (((1,), (1,)), ((), ())),
            preferred_element_type=jnp.float32,
        )
        for g in range(groups)
    ]
    p_ref[...] = jnp.concatenate(parts, axis=1).reshape(p_ref.shape)


def gram_kernel(p_ref, gram_ref):
    rank = gram_ref.shape[0]
    packed = p_ref[...]
    wide = lax.dot_general(
        packed, packed, (((0,), (0,)), ((), ())), precision=HIGHEST, preferred_element_type=jnp.float32
    )
    total = wide[:rank, :rank]
    for g in range(1, 128 // rank):
        total += wide[rank * g : rank * g + rank, rank * g : rank * g + rank]
    gram_ref[...] = total


def tiled_inverse_factor(gram, columns):
    rank = gram.shape[0]
    blocks = rank // 8
    for j in range(rank):
        column = jnp.broadcast_to(gram[:, j : j + 1], (rank, 128))
        for i in range(j // 8, blocks):
            columns[j, i] = column[8 * i : 8 * i + 8]
    row = lax.broadcasted_iota(jnp.int32, (8, 128), 0)
    lane = lax.broadcasted_iota(jnp.int32, (8, 128), 1) % rank
    solved = [(lane == row + 8 * i).astype(jnp.float32) for i in range(blocks)]
    for k in range(rank):
        top, at = k // 8, k % 8
        pivot = columns[k, top][at : at + 1]
        scale = lax.rsqrt(pivot)
        scale = scale * (1.5 - 0.5 * pivot * scale * scale)
        lower = {i: columns[k, i] * scale for i in range(top, blocks)}
        lower[top] = jnp.where(row > at, lower[top], 0.0)
        solved_row = solved[top][at : at + 1] * scale
        for i in range(top, blocks):
            reduced = solved[i] - lower[i] * solved_row
            solved[i] = jnp.where(row == at, solved_row, reduced) if i == top else reduced
        for j in range(k + 1, rank):
            entry = lower[j // 8][j % 8 : j % 8 + 1]
            for i in range(j // 8, blocks):
                columns[j, i] = columns[j, i] - lower[i] * entry
    return jnp.concatenate(solved, axis=0)


def basis_kernel(own_gram_ref, other_gram_ref, p_ref, p_own_ref, block_ref, q_ref, basis_ref, columns):
    chips, rows, width = block_ref.shape
    rank = own_gram_ref.shape[0]
    groups = 128 // rank
    per = rows // groups
    inverse = tiled_inverse_factor(own_gram_ref[...] + other_gram_ref[...], columns)
    tall = jnp.concatenate([inverse] * groups, axis=0)
    of_row = lax.broadcasted_iota(jnp.int32, (128, 128), 0) // rank
    of_lane = lax.broadcasted_iota(jnp.int32, (128, 128), 1) // rank
    diagonal = jnp.where(of_row == of_lane, tall, 0.0)
    over_lanes = (((1,), (1,)), ((), ()))
    basis = lax.dot_general(
        p_ref[...], diagonal, over_lanes, precision=HIGHEST, preferred_element_type=jnp.float32
    )
    own = lax.dot_general(
        p_own_ref[...], diagonal, over_lanes, precision=HIGHEST, preferred_element_type=jnp.float32
    )
    for g in range(groups):
        basis_ref[per * g : per * g + per, :] = own[:, rank * g : rank * g + rank]
    left = basis.T.astype(jnp.bfloat16)
    total = jnp.zeros((rank, width), jnp.float32)
    for g in range(groups):
        total += jnp.dot(
            left[rank * g : rank * g + rank],
            block_ref[:, per * g : per * g + per, :].reshape(chips * per, width),
            preferred_element_type=jnp.float32,
        )
    q_ref[...] = total


def gather_chips(values):
    by_hi = spread(values, "hi")
    return spread(by_hi, "lo").swapaxes(0, 1)


def gather_right(q_half):
    blocks = gather_chips(q_half)
    hi, lo, half, width = blocks.shape
    own = blocks.transpose(2, 0, 1, 3).reshape(half, hi * lo * width)
    return own, swap_cores(own)


def on_device(accumulated, q_start):
    own_rows = accumulated[0]
    replicas = lax.axis_size("rep")
    chips = lax.axis_size(CHIP)
    core = lax.axis_index("core")
    rows, cols = own_rows.shape
    rank, shard_cols = q_start.shape
    half, width, per = rank // 2, cols // chips, rows * rank // 128
    f32, bf16 = jnp.float32, jnp.bfloat16

    blocks = cut(own_rows, chips)
    block = lax.all_to_all(blocks, CHIP, 0, 0, tiled=True)

    shift = shard_cols % 128
    placed = jnp.where(
        core == 0, jnp.pad(q_start, ((0, 0), (0, shift))), jnp.pad(q_start, ((0, 0), (shift, 0)))
    )
    by_hi = exchanged(placed, "hi", 0)
    own = exchanged(by_hi, "lo", 1)
    other = swap_cores(own)
    p_own = kernel_call(
        first_p_kernel, jax.ShapeDtypeStruct((per, 128), f32), 2 * rows * rank * cols
    )(own, other, blocks)
    for iteration in range(ITERS):
        if iteration > 0:
            term = kernel_call(
                next_p_kernel, jax.ShapeDtypeStruct((chips, per, 128), f32), 2 * chips * rows * rank * width
            )(right_factor, block)
            p_own = jnp.sum(lax.all_to_all(term, CHIP, 0, 0, tiled=True), axis=0)
        if replicas > 1:
            p_own = lax.psum(p_own, "rep")
        if iteration > 0:
            p_chip = spread(p_own, CHIP)
        else:
            by_lo = exchanged(p_own, "lo", 0)
            p_chip = exchanged(by_lo, "hi", 0)
        p_rows = p_chip.reshape(chips * per, 128)
        own_gram = kernel_call(
            gram_kernel, jax.ShapeDtypeStruct((rank, rank), f32), 2 * chips * per * 128 * 128
        )(p_rows)
        q_term, basis = kernel_call(
            basis_kernel,
            (jax.ShapeDtypeStruct((rank, width), f32), jax.ShapeDtypeStruct((rows, rank), f32)),
            2 * chips * rows * rank * width,
            [pltpu.VMEM((rank, rank // 8, 8, 128), f32)],
        )(own_gram, swap_cores(own_gram), p_rows, p_own, block)
        q_chip = q_term + swap_cores(q_term)
        if replicas > 1:
            q_chip = lax.psum(q_chip, "rep")
        q_chip = q_chip / replicas
        right_factor = q_chip.astype(bf16)
    q_owned = lax.dynamic_slice_in_dim(q_chip, core * shard_cols, shard_cols, 1)
    own, other = gather_right(lax.dynamic_slice_in_dim(right_factor, core * half, half, 0))
    basis_bf16 = basis.astype(bf16)
    mine = lax.dynamic_slice_in_dim(basis_bf16, core * half, half, 1)
    theirs = lax.dynamic_slice_in_dim(basis_bf16, (1 - core) * half, half, 1)
    approx = lax.dot_general(
        jnp.concatenate([mine, theirs], axis=1),
        jnp.concatenate([own, other], axis=0),
        (((1,), (0,)), ((), ())),
        preferred_element_type=f32,
    )
    residual_buffer = (own_rows.astype(f32) - approx).astype(bf16)[None]
    return (residual_buffer, basis, q_owned)


def solution(mesh):
    chips = mesh.shape["fsdp"] // 2
    lo = 4
    split = Mesh(
        mesh.devices.reshape(mesh.shape["rep"], chips // lo, lo, 2), ("rep", "hi", "lo", "core")
    )
    in_specs = (P("rep", ROWS, None), P(None, ROWS))
    out_specs = (P("rep", ROWS, None), P(ROWS, None), P(None, ROWS))
    return jax.shard_map(
        on_device, mesh=split, in_specs=in_specs, out_specs=out_specs, check_vma=False
    )
```

time: 126 us -> 140 us (1.11)
  waiting for transfers between devices: 34.5 us -> 58.4 us
  local copies, waits for them, and re-layouts: 9.33 us -> 2.4 us
  Pallas kernels: 1.2 us -> 7.85 us
  matrix products: 7.67 us -> 1.92 us
  other arithmetic: 3.42 us -> 0.45 us
    ppermute x12, waiting for transfers between devices: 28.4 us -> 51.5 us  [exchanged(): pieces.append(lax.ppermute(values, axis, pairs))]
    pallas_call x2 -> x7, Pallas kernels: 1.2 us -> 7.85 us  [the longest x6 5.36 us: kernel_call(): pl.pallas_call(kernel, out_shape=out_shape, in_specs=[vmem] * len(args),...]
    dot_general x9 -> x0, matrix products: 5.78 us -> none  [the longest x2 3.01 us: product_transposed(): lax.dot_general(left, right, (((1,), (1,)), ((), ())), preferred_element_...]
    transpose x2 -> x0, local copies, waits for them, and re-layouts: 2.35 us -> none  [the longest x1 1.64 us: on_device(): blocks = own_rows.reshape(rows, chips, width).transpose(1, 0, 2)]
    reshape x5 -> x0, local copies, waits for them, and re-layouts: 2.2 us -> none  [the longest x1 1.62 us: on_device(): start = (even + odd).transpose(2, 0, 1, 3).reshape(rank, cols)]
    all_to_all x2 -> x0, other arithmetic: 1.9 us -> none  [the longest x1 0.95 us: spread(): return lax.all_to_all(copies, axis, 0, 0, tiled=True)]
    unnamed x10 -> x7, local copies, waits for them, and re-layouts: 2.34 us -> 0.7 us
  transfers between devices with their start and end apart: 19 -> 19, of which waited for: 13 -> 16; matrix products, arithmetic and copies ran while one was open for 9% -> 1% of each run, Pallas kernels for 0% -> 1%
where the time goes in v4:
time: 140 us; the launch traced here: 139 us
  waiting for transfers between devices  58.4 us (42%)
  blocking collectives  42 us (30%)
  starting transfers between devices  25.4 us (18%)
  Pallas kernels  7.85 us (6%)
  local copies, waits for them, and re-layouts  2.4 us (2%)
  matrix products  1.92 us (1%)
    ppermute x12, waiting for transfers between devices, exchanged(): pieces.append(lax.ppermute(values, axis, pairs))  51.5 us
    all_to_all x3, blocking collectives, spread(): return lax.all_to_all(copies, axis, 0, 0, tiled=True)  29.1 us
    ppermute x12, starting transfers between devices, exchanged(): pieces.append(lax.ppermute(values, axis, pairs))  16.4 us
    all_to_all x1, blocking collectives, on_device(): p_own = jnp.sum(lax.all_to_all(term, CHIP, 0, 0, tiled=True), axis=0)  13 us
    all_to_all x1, starting transfers between devices, on_device(): block = lax.all_to_all(blocks, CHIP, 0, 0, tiled=True)  8.35 us
    ppermute x6, waiting for transfers between devices, swap_cores(): return lax.ppermute(values, 'core', SWAP)  6.86 us
    pallas_call x6, Pallas kernels, kernel_call(): pl.pallas_call(kernel, out_shape=out_shape, in_specs=[vmem] * len(args),...  5.36 us
  transfers between devices with their start and end apart: 19, of which 16 were waited for; matrix products, arithmetic and copies ran while one was open for 1% of the time, Pallas kernels for 1%

profile of v4, /device:TPU:0, one launch (start us, length us, event | category | flops | bytes accessed | tf_op | source)
XLA Modules:
  0.0 139.3 jit_solution(9357352880635361497)
XLA Ops:
  0.6 2.5 %cut.1.blocks_ref = bf16[16,64,896]{2,1,0:T(8,128)(2,1)} custom-call(bf16[64,14336]{1,0:T(8,128)(2,1)} %bitcast.49), custom_call_target="tpu_custom_call" | custom-call | flops 1000 | bytes 3670016 | tf_op jit(solution)/shard_map/cut/pallas_call | solution.py:88
  3.1 0.0 copy-start.2
  3.1 8.4 %all-to-all-start = ((bf16[16,64,896]{2,1,0:T(8,128)(2,1)}), bf16[16,64,896]{2,1,0:T(8,128)(2,1)S(1)}, u32[]{:S(2)}, u32[]{:S(2)}) async-start(bf16[16,64,896]{2,1,0:T(8,128)(2,1)} %cut.1.blocks_ref), calls=%async_computation | async-start | bytes 3670016 | tf_op jit(solution)/shard_map/all_to_all | solution.py:235
  11.5 0.0 copy-done.2
  11.5 0.1 pad_select_fusion
  11.6 2.0 %collective-permute-start.2 = (bf16[32,512]{1,0:T(8,128)(2,1)S(1)}, bf16[32,512]{1,0:T(8,128)(2,1)S(1)}, u32[]{:S(2)}, u32[]{:S(2)}) collective-permute-start(bf16[32,512]{1,0:T(8,128)(2,1)S(1)} %pad_select_fusion), channel_id=1, source_target_pairs={{0,8},{8,0},{16,24},{24,16},{1,9},{9,1},{17,25},{25,17},{2,10},{10... | collective-permute-start | bytes 98312 | tf_op jit(solution)/shard_map/ppermute | solution.py:31
  13.6 2.4 %collective-permute-start.1 = (bf16[32,512]{1,0:T(8,128)(2,1)S(1)}, bf16[32,512]{1,0:T(8,128)(2,1)S(1)}, u32[]{:S(2)}, u32[]{:S(2)}) collective-permute-start(bf16[32,512]{1,0:T(8,128)(2,1)S(1)} %pad_select_fusion), channel_id=1, source_target_pairs={{0,16},{8,24},{16,0},{24,8},{1,17},{9,25},{17,1},{25,9},{2,18},{10... | collective-permute-start | bytes 98312 | tf_op jit(solution)/shard_map/ppermute | solution.py:31
  15.9 0.1 collective-permute-start
  16.0 26.6 %collective-permute-done.2 = bf16[32,512]{1,0:T(8,128)(2,1)S(1)} collective-permute-done((bf16[32,512]{1,0:T(8,128)(2,1)S(1)}, bf16[32,512]{1,0:T(8,128)(2,1)S(1)}, u32[]{:S(2)}, u32[]{:S(2)}) %collective-permute-start.2) | collective-permute-done | bytes 32800 | tf_op jit(solution)/shard_map/ppermute | solution.py:31
  42.6 13.9 %collective-permute-done.1 = bf16[32,512]{1,0:T(8,128)(2,1)S(1)} collective-permute-done((bf16[32,512]{1,0:T(8,128)(2,1)S(1)}, bf16[32,512]{1,0:T(8,128)(2,1)S(1)}, u32[]{:S(2)}, u32[]{:S(2)}) %collective-permute-start.1) | collective-permute-done | bytes 32800 | tf_op jit(solution)/shard_map/ppermute | solution.py:31
  56.5 0.0 collective-permute-done
  56.5 0.1 select_bitcast_fusion.11
  56.7 1.5 %collective-permute-start.5 = (bf16[4,32,512]{2,1,0:T(8,128)(2,1)S(1)}, bf16[4,32,512]{2,1,0:T(8,128)(2,1)S(1)}, u32[]{:S(2)}, u32[]{:S(2)}) collective-permute-start(bf16[4,32,512]{2,1,0:T(8,128)(2,1)S(1)} %pad_maximum_fusion.1), channel_id=1, source_target_pairs={{0,2},{2,0},{4,6},{6,4},{1,3},{3,1},{5,7},{7,5},{8,10},{10,8},{12,... | collective-permute-start | bytes 393224 | tf_op jit(solution)/shard_map/ppermute | solution.py:31
  58.2 2.0 %collective-permute-start.4 = (bf16[4,32,512]{2,1,0:T(8,128)(2,1)S(1)}, bf16[4,32,512]{2,1,0:T(8,128)(2,1)S(1)}, u32[]{:S(2)}, u32[]{:S(2)}) collective-permute-start(bf16[4,32,512]{2,1,0:T(8,128)(2,1)S(1)} %pad_maximum_fusion.1), channel_id=1, source_target_pairs={{0,4},{2,6},{4,0},{6,2},{1,5},{3,7},{5,1},{7,3},{8,12},{10,14},{12... | collective-permute-start | bytes 393224 | tf_op jit(solution)/shard_map/ppermute | solution.py:31
  60.1 0.6 collective-permute-start.3
  60.7 2.3 %collective-permute-done.5 = bf16[4,32,512]{2,1,0:T(8,128)(2,1)S(1)} collective-permute-done((bf16[4,32,512]{2,1,0:T(8,128)(2,1)S(1)}, bf16[4,32,512]{2,1,0:T(8,128)(2,1)S(1)}, u32[]{:S(2)}, u32[]{:S(2)}) %collective-permute-start.5) | collective-permute-done | bytes 131104 | tf_op jit(solution)/shard_map/ppermute | solution.py:31
  63.0 1.5 %collective-permute-done.4 = bf16[4,32,512]{2,1,0:T(8,128)(2,1)S(1)} collective-permute-done((bf16[4,32,512]{2,1,0:T(8,128)(2,1)S(1)}, bf16[4,32,512]{2,1,0:T(8,128)(2,1)S(1)}, u32[]{:S(2)}, u32[]{:S(2)}) %collective-permute-start.4) | collective-permute-done | bytes 131104 | tf_op jit(solution)/shard_map/ppermute | solution.py:31
  64.5 1.5 %collective-permute-done.3 = bf16[4,32,512]{2,1,0:T(8,128)(2,1)S(1)} collective-permute-done((bf16[4,32,512]{2,1,0:T(8,128)(2,1)S(1)}, bf16[4,32,512]{2,1,0:T(8,128)(2,1)S(1)}, u32[]{:S(2)}, u32[]{:S(2)}) %collective-permute-start.3) | collective-permute-done | bytes 131104 | tf_op jit(solution)/shard_map/ppermute | solution.py:31
  66.0 0.1 select_bitcast_fusion.3
  66.1 0.1 pad_maximum_fusion.own_ref
  66.2 0.1 collective-permute-start.6
  66.3 1.9 %collective-permute-done.6.other_ref = bf16[4,4,32,512]{3,2,1,0:T(8,128)(2,1)S(1)} collective-permute-done((bf16[4,4,32,512]{3,2,1,0:T(8,128)(2,1)S(1)}, bf16[4,4,32,512]{3,2,1,0:T(8,128)(2,1)S(1)}, u32[]{:S(2)}, u32[]{:S(2)}) %collective-permute-start.6) | collective-permute-done | bytes 524320 | tf_op jit(solution)/shard_map/ppermute | solution.py:17
  68.2 0.0 copy-done
  68.2 0.8 shard_map.49.p_own_ref
  68.9 1.1 collective-permute-start.9
  70.0 0.8 collective-permute-start.8
  70.9 1.5 %collective-permute-start.7 = (f32[16,128]{1,0:T(8,128)S(1)}, f32[16,128]{1,0:T(8,128)S(1)}, u32[]{:S(2)}, u32[]{:S(2)}) collective-permute-start(f32[16,128]{1,0:T(8,128)S(1)} %shard_map.49.p_own_ref), channel_id=1, source_target_pairs={{0,6},{2,4},{4,2},{6,0},{1,7},{3,5},{5,3},{7,1},{8,14},{10,12},{12... | collective-permute-start | bytes 24584 | tf_op jit(solution)/shard_map/ppermute | solution.py:31
  72.4 0.2 collective-permute-done.9
  72.6 1.1 collective-permute-done.8
  73.7 1.7 %collective-permute-done.7 = f32[16,128]{1,0:T(8,128)S(1)} collective-permute-done((f32[16,128]{1,0:T(8,128)S(1)}, f32[16,128]{1,0:T(8,128)S(1)}, u32[]{:S(2)}, u32[]{:S(2)}) %collective-permute-start.7) | collective-permute-done | bytes 8224 | tf_op jit(solution)/shard_map/ppermute | solution.py:31
  75.5 1.4 %collective-permute-start.12 = (f32[4,16,128]{2,1,0:T(8,128)S(1)}, f32[4,16,128]{2,1,0:T(8,128)S(1)}, u32[]{:S(2)}, u32[]{:S(2)}) collective-permute-start(f32[4,16,128]{2,1,0:T(8,128)S(1)} %pad_maximum_fusion.3), channel_id=1, source_target_pairs={{0,8},{8,0},{16,24},{24,16},{1,9},{9,1},{17,25},{25,17},{2,10},{10... | collective-permute-start | bytes 98312 | tf_op jit(solution)/shard_map/ppermute | solution.py:31
  76.9 0.0 collective-permute-start.11
  76.9 3.0 %collective-permute-start.10 = (f32[4,16,128]{2,1,0:T(8,128)S(1)}, f32[4,16,128]{2,1,0:T(8,128)S(1)}, u32[]{:S(2)}, u32[]{:S(2)}) collective-permute-start(f32[4,16,128]{2,1,0:T(8,128)S(1)} %pad_maximum_fusion.3), channel_id=1, source_target_pairs={{0,24},{8,16},{16,8},{24,0},{1,25},{9,17},{17,9},{25,1},{2,26},{10... | collective-permute-start | bytes 98312 | tf_op jit(solution)/shard_map/ppermute | solution.py:31
  79.9 0.0 collective-permute-done.12
  79.9 2.1 %collective-permute-done.11 = f32[4,16,128]{2,1,0:T(8,128)S(1)} collective-permute-done((f32[4,16,128]{2,1,0:T(8,128)S(1)}, f32[4,16,128]{2,1,0:T(8,128)S(1)}, u32[]{:S(2)}, u32[]{:S(2)}) %collective-permute-start.11) | collective-permute-done | bytes 32800 | tf_op jit(solution)/shard_map/ppermute | solution.py:31
  82.1 0.6 collective-permute-done.10
  82.7 0.4 shard_map.50.own_gram_ref
  83.0 0.1 collective-permute-start.13
  83.1 1.2 collective-permute-done.13.other_gram_ref
  84.3 0.0 all-to-all-done.block_ref
  84.3 1.7 %shard_map.51 = (f32[32,896]{1,0:T(8,128)S(1)}, f32[64,32]{1,0:T(8,128)}) custom-call(f32[32,32]{1,0:T(8,128)S(1)} %shard_map.50.own_gram_ref, f32[32,32]{1,0:T(8,128)S(1)} %collective-permute-done.13.other_gram_ref, f32[256,128]{1,0:T(8,128)S(1)} %bitcast.46, f32[16,128]{1,0:T(8,128)S(1)} %shard_map.49.p_own_ref, ...), custom_call_target="tpu_custom_call" | custom-call | flops 58720256 | bytes 1982464 | tf_op jit(solution)/shard_map/pallas_call | solution.py:44
  86.0 0.2 collective-permute-start.14
  86.2 1.2 collective-permute-done.14
  87.4 0.7 shard_map.52
  88.1 13.0 %all_to_all.25 = f32[16,16,128]{2,1,0:T(8,128)S(1)} all-to-all(f32[16,16,128]{2,1,0:T(8,128)S(1)} %shard_map.52), channel_id=1, replica_groups=mesh['rep'=1,'hi'=4,'lo'=4,'core'=2] {'hi','lo'}, dimensions={0} | all-to-all | bytes 262144 | tf_op jit(solution)/shard_map/all_to_all | solution.py:252
  101.1 10.7 %all_to_all.26 = f32[16,16,128]{2,1,0:T(8,128)S(1)} all-to-all(f32[16,16,128]{2,1,0:T(8,128)S(1)} %broadcast_in_dim.8), channel_id=1, replica_groups=mesh['rep'=1,'hi'=4,'lo'=4,'core'=2] {'hi','lo'}, dimensions={0} | all-to-all | bytes 262144 | tf_op jit(solution)/shard_map/all_to_all | solution.py:22
  111.8 0.4 shard_map.53.own_gram_ref
  112.2 0.1 collective-permute-start.15
  112.2 1.2 collective-permute-done.15.other_gram_ref
  113.4 1.4 %shard_map.54 = (f32[32,896]{1,0:T(8,128)S(1)}, f32[64,32]{1,0:T(8,128)S(1)}) custom-call(f32[32,32]{1,0:T(8,128)S(1)} %shard_map.53.own_gram_ref, f32[32,32]{1,0:T(8,128)S(1)} %collective-permute-done.15.other_gram_ref, f32[256,128]{1,0:T(8,128)S(1)} %bitcast.48, f32[16,128]{1,0:T(8,128)S(1)} %reduce_sum.9.p_own_ref, ...), custom_call_target="tpu_custom_call" | custom-call | flops 58720256 | bytes 1982464 | tf_op jit(solution)/shard_map/pallas_call | solution.py:44
  114.9 0.2 collective-permute-start.16
  115.1 1.2 collective-permute-done.16
  116.3 8.6 %all_to_all.27 = bf16[4,16,896]{2,1,0:T(8,128)(2,1)S(1)} all-to-all(bf16[4,16,896]{2,1,0:T(8,128)(2,1)S(1)} %broadcast_in_dim.9), channel_id=1, replica_groups=mesh['rep'=1,'hi'=4,'lo'=4,'core'=2] {'hi'}, dimensions={0} | all-to-all | bytes 229376 | tf_op jit(solution)/shard_map/all_to_all | solution.py:22
  124.9 0.0 copy-start.1
  124.9 0.1 broadcast_in_dim.10
  125.1 9.7 %all_to_all.28 = bf16[4,4,16,896]{3,1,2,0:T(4,128)(2,1)S(1)} all-to-all(bf16[4,4,16,896]{3,1,2,0:T(4,128)(2,1)S(1)} %broadcast_in_dim.10), channel_id=1, replica_groups=mesh['rep'=1,'hi'=4,'lo'=4,'core'=2] {'lo'}, dimensions={0} | all-to-all | bytes 917504 | tf_op jit(solution)/shard_map/all_to_all | solution.py:22
  134.8 0.4 copy.17
  135.2 0.3 reshape.20
  135.5 0.1 collective-permute-start.17
  135.6 0.7 copy.18
  136.3 0.1 constant_dynamic-slice_fusion.2
  136.4 0.7 constant_dynamic-slice_fusion
  137.1 0.3 collective-permute-done.17
  137.4 1.9 %fusion.1 = bf16[1,64,14336]{2,1,0:T(8,128)(2,1)} fusion(bf16[16,14336]{1,0:T(8,128)(2,1)S(1)} %collective-permute-done.17, bf16[16,14336]{1,0:T(8,128)(2,1)S(1)} %reshape.20, bf16[64,16]{1,0:T(8,128)(2,1)S(1)} %get-tuple-element.33, bf16[64,16]{1,0:T(8,128)(2,1)S(1)} %get-tuple-element.32, bf16[1,64,14336]{2,1,0:T(8,128)(2,1)S(1)} %copy-done.1), kind=kOutput, calls=%fused_computation.2 | convolution fusion | flops 63315968 | bytes 4591616 | tf_op jit(solution)/shard_map/dot_general | solution.py:280
  (17 shorter events, 0.2 us)
Async XLA Ops:
  3.1 8.4 %copy-start.2 = (bf16[32,448]{1,0:T(8,128)(2,1)S(1)}, bf16[32,448]{1,0:T(8,128)(2,1)}, u32[]{:S(2)}) copy-start(bf16[32,448]{1,0:T(8,128)(2,1)} %param.3) | copy-start | bytes 86020
  3.1 81.2 %all-to-all-start = ((bf16[16,64,896]{2,1,0:T(8,128)(2,1)}), bf16[16,64,896]{2,1,0:T(8,128)(2,1)S(1)}, u32[]{:S(2)}, u32[]{:S(2)}) async-start(bf16[16,64,896]{2,1,0:T(8,128)(2,1)} %cut.1.blocks_ref), calls=%async_computation | async-start | bytes 3670016 | tf_op jit(solution)/shard_map/all_to_all | solution.py:235
  11.6 31.0 %collective-permute-start.2 = (bf16[32,512]{1,0:T(8,128)(2,1)S(1)}, bf16[32,512]{1,0:T(8,128)(2,1)S(1)}, u32[]{:S(2)}, u32[]{:S(2)}) collective-permute-start(bf16[32,512]{1,0:T(8,128)(2,1)S(1)} %pad_select_fusion), channel_id=1, source_target_pairs={{0,8},{8,0},{16,24},{24,16},{1,9},{9,1},{17,25},{25,17},{2,10},{10... | collective-permute-start | bytes 98312 | tf_op jit(solution)/shard_map/ppermute | solution.py:31
  13.6 43.0 %collective-permute-start.1 = (bf16[32,512]{1,0:T(8,128)(2,1)S(1)}, bf16[32,512]{1,0:T(8,128)(2,1)S(1)}, u32[]{:S(2)}, u32[]{:S(2)}) collective-permute-start(bf16[32,512]{1,0:T(8,128)(2,1)S(1)} %pad_select_fusion), channel_id=1, source_target_pairs={{0,16},{8,24},{16,0},{24,8},{1,17},{9,25},{17,1},{25,9},{2,18},{10... | collective-permute-start | bytes 98312 | tf_op jit(solution)/shard_map/ppermute | solution.py:31
  15.9 40.6 %collective-permute-start = (bf16[32,512]{1,0:T(8,128)(2,1)S(1)}, bf16[32,512]{1,0:T(8,128)(2,1)S(1)}, u32[]{:S(2)}, u32[]{:S(2)}) collective-permute-start(bf16[32,512]{1,0:T(8,128)(2,1)S(1)} %pad_select_fusion), channel_id=1, source_target_pairs={{0,24},{8,16},{16,8},{24,0},{1,25},{9,17},{17,9},{25,1},{2,26},{10... | collective-permute-start | bytes 98312 | tf_op jit(solution)/shard_map/ppermute | solution.py:31
  56.7 6.4 %collective-permute-start.5 = (bf16[4,32,512]{2,1,0:T(8,128)(2,1)S(1)}, bf16[4,32,512]{2,1,0:T(8,128)(2,1)S(1)}, u32[]{:S(2)}, u32[]{:S(2)}) collective-permute-start(bf16[4,32,512]{2,1,0:T(8,128)(2,1)S(1)} %pad_maximum_fusion.1), channel_id=1, source_target_pairs={{0,2},{2,0},{4,6},{6,4},{1,3},{3,1},{5,7},{7,5},{8,10},{10,8},{12,... | collective-permute-start | bytes 393224 | tf_op jit(solution)/shard_map/ppermute | solution.py:31
  58.2 6.3 %collective-permute-start.4 = (bf16[4,32,512]{2,1,0:T(8,128)(2,1)S(1)}, bf16[4,32,512]{2,1,0:T(8,128)(2,1)S(1)}, u32[]{:S(2)}, u32[]{:S(2)}) collective-permute-start(bf16[4,32,512]{2,1,0:T(8,128)(2,1)S(1)} %pad_maximum_fusion.1), channel_id=1, source_target_pairs={{0,4},{2,6},{4,0},{6,2},{1,5},{3,7},{5,1},{7,3},{8,12},{10,14},{12... | collective-permute-start | bytes 393224 | tf_op jit(solution)/shard_map/ppermute | solution.py:31
  60.1 5.9 %collective-permute-start.3 = (bf16[4,32,512]{2,1,0:T(8,128)(2,1)S(1)}, bf16[4,32,512]{2,1,0:T(8,128)(2,1)S(1)}, u32[]{:S(2)}, u32[]{:S(2)}) collective-permute-start(bf16[4,32,512]{2,1,0:T(8,128)(2,1)S(1)} %pad_maximum_fusion.1), channel_id=1, source_target_pairs={{0,6},{2,4},{4,2},{6,0},{1,7},{3,5},{5,3},{7,1},{8,14},{10,12},{12... | collective-permute-start | bytes 393224 | tf_op jit(solution)/shard_map/ppermute | solution.py:31
  60.7 7.5 %copy-start = (bf16[16,64,896]{2,1,0:T(8,128)(2,1)S(1)}, bf16[16,64,896]{2,1,0:T(8,128)(2,1)}, u32[]{:S(2)}) copy-start(bf16[16,64,896]{2,1,0:T(8,128)(2,1)} %cut.1.blocks_ref) | copy-start | bytes 5505028
  66.2 2.0 %collective-permute-start.6 = (bf16[4,4,32,512]{3,2,1,0:T(8,128)(2,1)S(1)}, bf16[4,4,32,512]{3,2,1,0:T(8,128)(2,1)S(1)}, u32[]{:S(2)}, u32[]{:S(2)}) collective-permute-start(bf16[4,4,32,512]{3,2,1,0:T(8,128)(2,1)S(1)} %pad_maximum_fusion.own_ref), channel_id=1, source_target_pairs={{0,1},{1,0},{2,3},{3,2},{4,5},{5,4},{6,7},{7,6},{8,9},{9,8},{10,11... | collective-permute-start | bytes 1572872 | tf_op jit(solution)/shard_map/ppermute | solution.py:17
  68.9 3.7 %collective-permute-start.9 = (f32[16,128]{1,0:T(8,128)S(1)}, f32[16,128]{1,0:T(8,128)S(1)}, u32[]{:S(2)}, u32[]{:S(2)}) collective-permute-start(f32[16,128]{1,0:T(8,128)S(1)} %shard_map.49.p_own_ref), channel_id=1, source_target_pairs={{0,2},{2,0},{4,6},{6,4},{1,3},{3,1},{5,7},{7,5},{8,10},{10,8},{12,... | collective-permute-start | bytes 24584 | tf_op jit(solution)/shard_map/ppermute | solution.py:31
  70.0 3.7 %collective-permute-start.8 = (f32[16,128]{1,0:T(8,128)S(1)}, f32[16,128]{1,0:T(8,128)S(1)}, u32[]{:S(2)}, u32[]{:S(2)}) collective-permute-start(f32[16,128]{1,0:T(8,128)S(1)} %shard_map.49.p_own_ref), channel_id=1, source_target_pairs={{0,4},{2,6},{4,0},{6,2},{1,5},{3,7},{5,1},{7,3},{8,12},{10,14},{12... | collective-permute-start | bytes 24584 | tf_op jit(solution)/shard_map/ppermute | solution.py:31
  70.9 4.5 %collective-permute-start.7 = (f32[16,128]{1,0:T(8,128)S(1)}, f32[16,128]{1,0:T(8,128)S(1)}, u32[]{:S(2)}, u32[]{:S(2)}) collective-permute-start(f32[16,128]{1,0:T(8,128)S(1)} %shard_map.49.p_own_ref), channel_id=1, source_target_pairs={{0,6},{2,4},{4,2},{6,0},{1,7},{3,5},{5,3},{7,1},{8,14},{10,12},{12... | collective-permute-start | bytes 24584 | tf_op jit(solution)/shard_map/ppermute | solution.py:31
  75.5 4.5 %collective-permute-start.12 = (f32[4,16,128]{2,1,0:T(8,128)S(1)}, f32[4,16,128]{2,1,0:T(8,128)S(1)}, u32[]{:S(2)}, u32[]{:S(2)}) collective-permute-start(f32[4,16,128]{2,1,0:T(8,128)S(1)} %pad_maximum_fusion.3), channel_id=1, source_target_pairs={{0,8},{8,0},{16,24},{24,16},{1,9},{9,1},{17,25},{25,17},{2,10},{10... | collective-permute-start | bytes 98312 | tf_op jit(solution)/shard_map/ppermute | solution.py:31
  76.9 5.2 %collective-permute-start.11 = (f32[4,16,128]{2,1,0:T(8,128)S(1)}, f32[4,16,128]{2,1,0:T(8,128)S(1)}, u32[]{:S(2)}, u32[]{:S(2)}) collective-permute-start(f32[4,16,128]{2,1,0:T(8,128)S(1)} %pad_maximum_fusion.3), channel_id=1, source_target_pairs={{0,16},{8,24},{16,0},{24,8},{1,17},{9,25},{17,1},{25,9},{2,18},{10... | collective-permute-start | bytes 98312 | tf_op jit(solution)/shard_map/ppermute | solution.py:31
  76.9 5.7 %collective-permute-start.10 = (f32[4,16,128]{2,1,0:T(8,128)S(1)}, f32[4,16,128]{2,1,0:T(8,128)S(1)}, u32[]{:S(2)}, u32[]{:S(2)}) collective-permute-start(f32[4,16,128]{2,1,0:T(8,128)S(1)} %pad_maximum_fusion.3), channel_id=1, source_target_pairs={{0,24},{8,16},{16,8},{24,0},{1,25},{9,17},{17,9},{25,1},{2,26},{10... | collective-permute-start | bytes 98312 | tf_op jit(solution)/shard_map/ppermute | solution.py:31
  83.0 1.2 collective-permute-start.13
  86.0 1.3 collective-permute-start.14
  112.2 1.2 collective-permute-start.15
  114.9 1.4 collective-permute-start.16
  124.9 12.5 %copy-start.1 = (bf16[1,64,14336]{2,1,0:T(8,128)(2,1)S(1)}, bf16[1,64,14336]{2,1,0:T(8,128)(2,1)}, u32[]{:S(2)}) copy-start(bf16[1,64,14336]{2,1,0:T(8,128)(2,1)} %param.2) | copy-start | bytes 5505028
  135.5 1.9 %collective-permute-start.17 = (bf16[16,14336]{1,0:T(8,128)(2,1)S(1)}, bf16[16,14336]{1,0:T(8,128)(2,1)S(1)}, u32[]{:S(2)}, u32[]{:S(2)}) collective-permute-start(bf16[16,14336]{1,0:T(8,128)(2,1)S(1)} %reshape.20), channel_id=1, source_target_pairs={{0,1},{1,0},{2,3},{3,2},{4,5},{5,4},{6,7},{7,6},{8,9},{9,8},{10,11... | collective-permute-start | bytes 1376264 | tf_op jit(solution)/shard_map/ppermute | solution.py:17

commit v5 on v4

--- a/solution.py
+++ b/solution.py
@@ -101,9 +101,11 @@
     )(own_rows)
 
 
-def first_p_kernel(own_ref, other_ref, blocks_ref, p_ref):
-    chips, rows, width = blocks_ref.shape
-    _, lo, rank, placed = own_ref.shape
+def first_p_kernel(own_ref, other_ref, rows_ref, p_ref):
+    rows, cols = rows_ref.shape
+    hi, lo, rank, placed = own_ref.shape
+    chips = hi * lo
+    width = cols // chips
     rest = width - placed
     is_even = lax.axis_index("core") == 0
     total = jnp.zeros((rows, rank), jnp.float32)
@@ -113,7 +115,7 @@
         odd = jnp.where(is_even, other, own)
         for part, start in ((even, 0), (odd, rest)):
             total += lax.dot_general(
-                blocks_ref[chip, :, start : start + placed],
+                rows_ref[:, width * chip + start : width * chip + start + placed],
                 part,
                 (((1,), (1,)), ((), ())),
                 preferred_element_type=jnp.float32,
@@ -179,25 +181,28 @@
     return jnp.concatenate(solved, axis=0)
 
 
-def basis_kernel(own_gram_ref, other_gram_ref, p_ref, p_own_ref, block_ref, q_ref, basis_ref, columns):
+def diagonal_of(inverse, groups):
+    rank = inverse.shape[0]
+    tall = jnp.concatenate([inverse] * groups, axis=0)
+    of_row = lax.broadcasted_iota(jnp.int32, (128, 128), 0) // rank
+    of_lane = lax.broadcasted_iota(jnp.int32, (128, 128), 1) // rank
+    return jnp.where(of_row == of_lane, tall, 0.0)
+
+
+def basis_kernel(own_gram_ref, other_gram_ref, p_ref, block_ref, q_ref, inverse_ref, columns):
     chips, rows, width = block_ref.shape
     rank = own_gram_ref.shape[0]
     groups = 128 // rank
     per = rows // groups
     inverse = tiled_inverse_factor(own_gram_ref[...] + other_gram_ref[...], columns)
-    tall = jnp.concatenate([inverse] * groups, axis=0)
-    of_row = lax.broadcasted_iota(jnp.int32, (128, 128), 0) // rank
-    of_lane = lax.broadcasted_iota(jnp.int32, (128, 128), 1) // rank
-    diagonal = jnp.where(of_row == of_lane, tall, 0.0)
-    over_lanes = (((1,), (1,)), ((), ()))
+    inverse_ref[...] = inverse
     basis = lax.dot_general(
-        p_ref[...], diagonal, over_lanes, precision=HIGHEST, preferred_element_type=jnp.float32
-    )
-    own = lax.dot_general(
-        p_own_ref[...], diagonal, over_lanes, precision=HIGHEST, preferred_element_type=jnp.float32
-    )
-    for g in range(groups):
-        basis_ref[per * g : per * g + per, :] = own[:, rank * g : rank * g + rank]
+        p_ref[...],
+        diagonal_of(inverse, groups),
+        (((1,), (1,)), ((), ())),
+        precision=HIGHEST,
+        preferred_element_type=jnp.float32,
+    )
     left = basis.T.astype(jnp.bfloat16)
     total = jnp.zeros((rank, width), jnp.float32)
     for g in range(groups):
@@ -209,16 +214,102 @@
     q_ref[...] = total
 
 
-def gather_chips(values):
-    by_hi = spread(values, "hi")
-    return spread(by_hi, "lo").swapaxes(0, 1)
-
-
-def gather_right(q_half):
-    blocks = gather_chips(q_half)
-    hi, lo, half, width = blocks.shape
-    own = blocks.transpose(2, 0, 1, 3).reshape(half, hi * lo * width)
-    return own, swap_cores(own)
+def own_basis_kernel(inverse_ref, p_own_ref, basis_ref, rounded_ref):
+    rank = inverse_ref.shape[0]
+    groups = 128 // rank
+    own = lax.dot_general(
+        p_own_ref[...],
+        diagonal_of(inverse_ref[...], groups),
+        (((1,), (1,)), ((), ())),
+        precision=HIGHEST,
+        preferred_element_type=jnp.float32,
+    ).T
+    own = jnp.concatenate([own[rank * g : rank * g + rank] for g in range(groups)], axis=1)
+    basis_ref[...] = own
+    rounded_ref[...] = own.astype(rounded_ref.dtype)
+
+
+def fetch_kernel(rows_ref, held_ref, semaphores):
+    parts = semaphores.shape[0]
+    span = rows_ref.shape[0] // parts
+    copies = [
+        pltpu.make_async_copy(
+            rows_ref.at[span * i : span * i + span], held_ref.at[span * i : span * i + span], semaphores.at[i]
+        )
+        for i in range(parts)
+    ]
+    for copy in copies:
+        copy.start()
+    for copy in copies:
+        copy.wait()
+
+
+def fetch(own_rows):
+    parts = 4
+    return pl.pallas_call(
+        fetch_kernel,
+        out_shape=jax.ShapeDtypeStruct(own_rows.shape, own_rows.dtype),
+        in_specs=[pl.BlockSpec(memory_space=pltpu.HBM)],
+        out_specs=pl.BlockSpec(memory_space=pltpu.VMEM),
+        scratch_shapes=[pltpu.SemaphoreType.DMA((parts,))],
+        compiler_params=pltpu.CompilerParams(vmem_limit_bytes=54_000_000),
+        cost_estimate=pl.CostEstimate(
+            flops=1000000, bytes_accessed=2 * own_rows.size * own_rows.dtype.itemsize, transcendentals=0
+        ),
+        name="fetch",
+    )(own_rows)
+
+
+def residual_kernel(own_ref, other_ref, left_ref, q_ref, rows_ref, residual_ref, q_owned_ref, given, writes):
+    chips, _, width = own_ref.shape
+    parts, _, span = given.shape
+    shard_cols = q_owned_ref.shape[1]
+    copies = [
+        pltpu.make_async_copy(given.at[i], residual_ref.at[:, span * i : span * i + span], writes.at[i])
+        for i in range(parts)
+    ]
+    is_first = lax.axis_index("core") == 0
+    left = left_ref[...]
+    for i in range(parts):
+        for place in range(chips // parts):
+            chip = i * (chips // parts) + place
+            own, other = own_ref[chip], other_ref[chip]
+            right = jnp.concatenate(
+                [jnp.where(is_first, own, other), jnp.where(is_first, other, own)], axis=0
+            )
+            approx = lax.dot_general(
+                left, right, (((0,), (0,)), ((), ())), preferred_element_type=jnp.float32
+            )
+            kept = rows_ref[:, width * chip : width * chip + width].astype(jnp.float32)
+            given[i, :, width * place : width * place + width] = (kept - approx).astype(given.dtype)
+        copies[i].start()
+    q_owned_ref[...] = jnp.where(is_first, q_ref[:, :shard_cols], q_ref[:, shard_cols:])
+    for copy in copies:
+        copy.wait()
+
+
+def residual_and_columns(own, other, left, q_chip, own_rows, shard_cols):
+    rows, cols = own_rows.shape
+    parts = 8
+    vmem, hbm = pl.BlockSpec(memory_space=pltpu.VMEM), pl.BlockSpec(memory_space=pltpu.HBM)
+    return pl.pallas_call(
+        residual_kernel,
+        out_shape=(
+            jax.ShapeDtypeStruct((rows, cols), own_rows.dtype),
+            jax.ShapeDtypeStruct((q_chip.shape[0], shard_cols), jnp.float32),
+        ),
+        in_specs=[vmem] * 5,
+        out_specs=(hbm, vmem),
+        scratch_shapes=[
+            pltpu.VMEM((parts, rows, cols // parts), own_rows.dtype),
+            pltpu.SemaphoreType.DMA((parts,)),
+        ],
+        compiler_params=pltpu.CompilerParams(vmem_limit_bytes=16 * 1024 * 1024),
+        cost_estimate=pl.CostEstimate(
+            flops=2 * rows * cols * q_chip.shape[0], bytes_accessed=4 * rows * cols, transcendentals=0
+        ),
+        name="residual",
+    )(own, other, left, q_chip, own_rows)
 
 
 def on_device(accumulated, q_start):
@@ -243,7 +334,7 @@
     other = swap_cores(own)
     p_own = kernel_call(
         first_p_kernel, jax.ShapeDtypeStruct((per, 128), f32), 2 * rows * rank * cols
-    )(own, other, blocks)
+    )(own, other, own_rows)
     for iteration in range(ITERS):
         if iteration > 0:
             term = kernel_call(
@@ -261,30 +352,29 @@
         own_gram = kernel_call(
             gram_kernel, jax.ShapeDtypeStruct((rank, rank), f32), 2 * chips * per * 128 * 128
         )(p_rows)
-        q_term, basis = kernel_call(
+        q_term, inverse = kernel_call(
             basis_kernel,
-            (jax.ShapeDtypeStruct((rank, width), f32), jax.ShapeDtypeStruct((rows, rank), f32)),
+            (jax.ShapeDtypeStruct((rank, width), f32), jax.ShapeDtypeStruct((rank, 128), f32)),
             2 * chips * rows * rank * width,
             [pltpu.VMEM((rank, rank // 8, 8, 128), f32)],
-        )(own_gram, swap_cores(own_gram), p_rows, p_own, block)
+        )(own_gram, swap_cores(own_gram), p_rows, block)
         q_chip = q_term + swap_cores(q_term)
         if replicas > 1:
             q_chip = lax.psum(q_chip, "rep")
         q_chip = q_chip / replicas
         right_factor = q_chip.astype(bf16)
-    q_owned = lax.dynamic_slice_in_dim(q_chip, core * shard_cols, shard_cols, 1)
-    own, other = gather_right(lax.dynamic_slice_in_dim(right_factor, core * half, half, 0))
-    basis_bf16 = basis.astype(bf16)
-    mine = lax.dynamic_slice_in_dim(basis_bf16, core * half, half, 1)
-    theirs = lax.dynamic_slice_in_dim(basis_bf16, (1 - core) * half, half, 1)
-    approx = lax.dot_general(
-        jnp.concatenate([mine, theirs], axis=1),
-        jnp.concatenate([own, other], axis=0),
-        (((1,), (0,)), ((), ())),
-        preferred_element_type=f32,
-    )
-    residual_buffer = (own_rows.astype(f32) - approx).astype(bf16)[None]
-    return (residual_buffer, basis, q_owned)
+    basis, rounded = kernel_call(
+        own_basis_kernel,
+        (jax.ShapeDtypeStruct((rank, rows), f32), jax.ShapeDtypeStruct((rank, rows), bf16)),
+        2 * per * 128 * 128,
+    )(inverse, p_own)
+    own = spread(lax.dynamic_slice_in_dim(right_factor, core * half, half, 0)[None], CHIP)
+    own = own.reshape(chips, half, width)
+    own, later_rows = lax.optimization_barrier((own, own_rows))
+    residual, q_owned = residual_and_columns(
+        own, swap_cores(own), rounded, q_chip, fetch(later_rows), shard_cols
+    )
+    return (residual[None], basis.T, q_owned)
 
 
 def solution(mesh):

time: 140 us -> 138 us (0.986)
  Pallas kernels: 7.85 us -> 12.4 us
  local copies, waits for them, and re-layouts: 2.4 us -> 0.07 us
  matrix products: 1.92 us -> 0 us
    pallas_call x0 -> x2, Pallas kernels: none -> 3.62 us  [the longest x1 2.16 us: residual_and_columns(): pl.pallas_call(residual_kernel, out_shape=(jax.ShapeDtypeStruct((rows, co...]
    dot_general x1 -> x0, matrix products: 1.92 us -> none  [on_device(): lax.dot_general(jnp.concatenate([mine, theirs], axis=1), jnp.concatenate(...]
    all_to_all x3 -> x2, blocking collectives: 29.1 us -> 27.7 us  [spread(): return lax.all_to_all(copies, axis, 0, 0, tiled=True)]
    pallas_call x6 -> x7, Pallas kernels: 5.36 us -> 6.24 us  [kernel_call(): pl.pallas_call(kernel, out_shape=out_shape, in_specs=[vmem] * len(args),...]
  transfers between devices with their start and end apart: 19 -> 19, of which waited for: 16 -> 15; matrix products, arithmetic and copies ran while one was open for 1% -> 0% of each run, Pallas kernels for 1% -> 3%
where the time goes in v5:
time: 138 us
  waiting for transfers between devices  58.1 us (42%)
  blocking collectives  40.7 us (29%)
  starting transfers between devices  25.4 us (18%)
  Pallas kernels  12.4 us (9%)
    ppermute x12, waiting for transfers between devices, exchanged(): pieces.append(lax.ppermute(values, axis, pairs))  51.5 us
    all_to_all x2, blocking collectives, spread(): return lax.all_to_all(copies, axis, 0, 0, tiled=True)  27.7 us
    ppermute x12, starting transfers between devices, exchanged(): pieces.append(lax.ppermute(values, axis, pairs))  16.4 us
    all_to_all x1, blocking collectives, on_device(): p_own = jnp.sum(lax.all_to_all(term, CHIP, 0, 0, tiled=True), axis=0)  13 us
    all_to_all x1, starting transfers between devices, on_device(): block = lax.all_to_all(blocks, CHIP, 0, 0, tiled=True)  8.35 us
    ppermute x6, waiting for transfers between devices, swap_cores(): return lax.ppermute(values, 'core', SWAP)  6.56 us
    pallas_call x7, Pallas kernels, kernel_call(): pl.pallas_call(kernel, out_shape=out_shape, in_specs=[vmem] * len(args),...  6.24 us
  transfers between devices with their start and end apart: 19, of which 15 were waited for; matrix products, arithmetic and copies ran while one was open for 0% of the time, Pallas kernels for 3%

profile of v5, /device:TPU:0, one launch (start us, length us, event | category | flops | bytes accessed | tf_op | source)
XLA Modules:
  0.0 137.9 jit_solution(16201220383691884411)
XLA Ops:
  0.6 2.5 %cut.1 = bf16[16,64,896]{2,1,0:T(8,128)(2,1)} custom-call(bf16[64,14336]{1,0:T(8,128)(2,1)} %bitcast.44), custom_call_target="tpu_custom_call" | custom-call | flops 1000 | bytes 3670016 | tf_op jit(solution)/shard_map/cut/pallas_call | solution.py:88
  3.1 0.0 copy-start.1
  3.1 8.4 %all-to-all-start = ((bf16[16,64,896]{2,1,0:T(8,128)(2,1)}), bf16[16,64,896]{2,1,0:T(8,128)(2,1)S(1)}, u32[]{:S(2)}, u32[]{:S(2)}) async-start(bf16[16,64,896]{2,1,0:T(8,128)(2,1)} %cut.1), calls=%async_computation | async-start | bytes 3670016 | tf_op jit(solution)/shard_map/all_to_all | solution.py:326
  11.5 0.0 copy-done.1
  11.5 0.1 pad_select_fusion
  11.6 2.0 %collective-permute-start.2 = (bf16[32,512]{1,0:T(8,128)(2,1)S(1)}, bf16[32,512]{1,0:T(8,128)(2,1)S(1)}, u32[]{:S(2)}, u32[]{:S(2)}) collective-permute-start(bf16[32,512]{1,0:T(8,128)(2,1)S(1)} %pad_select_fusion), channel_id=1, source_target_pairs={{0,8},{8,0},{16,24},{24,16},{1,9},{9,1},{17,25},{25,17},{2,10},{10... | collective-permute-start | bytes 98312 | tf_op jit(solution)/shard_map/ppermute | solution.py:31
  13.6 2.4 %collective-permute-start.1 = (bf16[32,512]{1,0:T(8,128)(2,1)S(1)}, bf16[32,512]{1,0:T(8,128)(2,1)S(1)}, u32[]{:S(2)}, u32[]{:S(2)}) collective-permute-start(bf16[32,512]{1,0:T(8,128)(2,1)S(1)} %pad_select_fusion), channel_id=1, source_target_pairs={{0,16},{8,24},{16,0},{24,8},{1,17},{9,25},{17,1},{25,9},{2,18},{10... | collective-permute-start | bytes 98312 | tf_op jit(solution)/shard_map/ppermute | solution.py:31
  15.9 0.1 collective-permute-start
  16.0 26.6 %collective-permute-done.2 = bf16[32,512]{1,0:T(8,128)(2,1)S(1)} collective-permute-done((bf16[32,512]{1,0:T(8,128)(2,1)S(1)}, bf16[32,512]{1,0:T(8,128)(2,1)S(1)}, u32[]{:S(2)}, u32[]{:S(2)}) %collective-permute-start.2) | collective-permute-done | bytes 32800 | tf_op jit(solution)/shard_map/ppermute | solution.py:31
  42.6 13.9 %collective-permute-done.1 = bf16[32,512]{1,0:T(8,128)(2,1)S(1)} collective-permute-done((bf16[32,512]{1,0:T(8,128)(2,1)S(1)}, bf16[32,512]{1,0:T(8,128)(2,1)S(1)}, u32[]{:S(2)}, u32[]{:S(2)}) %collective-permute-start.1) | collective-permute-done | bytes 32800 | tf_op jit(solution)/shard_map/ppermute | solution.py:31
  56.5 0.0 collective-permute-done
  56.5 0.1 select_bitcast_fusion.11
  56.7 1.5 %collective-permute-start.5 = (bf16[4,32,512]{2,1,0:T(8,128)(2,1)S(1)}, bf16[4,32,512]{2,1,0:T(8,128)(2,1)S(1)}, u32[]{:S(2)}, u32[]{:S(2)}) collective-permute-start(bf16[4,32,512]{2,1,0:T(8,128)(2,1)S(1)} %pad_maximum_fusion.1), channel_id=1, source_target_pairs={{0,2},{2,0},{4,6},{6,4},{1,3},{3,1},{5,7},{7,5},{8,10},{10,8},{12,... | collective-permute-start | bytes 393224 | tf_op jit(solution)/shard_map/ppermute | solution.py:31
  58.2 2.0 %collective-permute-start.4 = (bf16[4,32,512]{2,1,0:T(8,128)(2,1)S(1)}, bf16[4,32,512]{2,1,0:T(8,128)(2,1)S(1)}, u32[]{:S(2)}, u32[]{:S(2)}) collective-permute-start(bf16[4,32,512]{2,1,0:T(8,128)(2,1)S(1)} %pad_maximum_fusion.1), channel_id=1, source_target_pairs={{0,4},{2,6},{4,0},{6,2},{1,5},{3,7},{5,1},{7,3},{8,12},{10,14},{12... | collective-permute-start | bytes 393224 | tf_op jit(solution)/shard_map/ppermute | solution.py:31
  60.1 0.6 collective-permute-start.3
  60.7 0.0 copy-start
  60.7 2.3 %collective-permute-done.5 = bf16[4,32,512]{2,1,0:T(8,128)(2,1)S(1)} collective-permute-done((bf16[4,32,512]{2,1,0:T(8,128)(2,1)S(1)}, bf16[4,32,512]{2,1,0:T(8,128)(2,1)S(1)}, u32[]{:S(2)}, u32[]{:S(2)}) %collective-permute-start.5) | collective-permute-done | bytes 131104 | tf_op jit(solution)/shard_map/ppermute | solution.py:31
  63.0 1.5 %collective-permute-done.4 = bf16[4,32,512]{2,1,0:T(8,128)(2,1)S(1)} collective-permute-done((bf16[4,32,512]{2,1,0:T(8,128)(2,1)S(1)}, bf16[4,32,512]{2,1,0:T(8,128)(2,1)S(1)}, u32[]{:S(2)}, u32[]{:S(2)}) %collective-permute-start.4) | collective-permute-done | bytes 131104 | tf_op jit(solution)/shard_map/ppermute | solution.py:31
  64.5 1.5 %collective-permute-done.3 = bf16[4,32,512]{2,1,0:T(8,128)(2,1)S(1)} collective-permute-done((bf16[4,32,512]{2,1,0:T(8,128)(2,1)S(1)}, bf16[4,32,512]{2,1,0:T(8,128)(2,1)S(1)}, u32[]{:S(2)}, u32[]{:S(2)}) %collective-permute-start.3) | collective-permute-done | bytes 131104 | tf_op jit(solution)/shard_map/ppermute | solution.py:31
  66.0 0.1 select_bitcast_fusion.3
  66.1 0.1 pad_maximum_fusion.own_ref
  66.2 0.1 collective-permute-start.6
  66.3 1.9 %collective-permute-done.6.other_ref = bf16[4,4,32,512]{3,2,1,0:T(8,128)(2,1)S(1)} collective-permute-done((bf16[4,4,32,512]{3,2,1,0:T(8,128)(2,1)S(1)}, bf16[4,4,32,512]{3,2,1,0:T(8,128)(2,1)S(1)}, u32[]{:S(2)}, u32[]{:S(2)}) %collective-permute-start.6) | collective-permute-done | bytes 524320 | tf_op jit(solution)/shard_map/ppermute | solution.py:17
  68.2 0.0 copy-done
  68.2 0.8 shard_map.49
  68.9 1.1 collective-permute-start.9
  70.1 0.8 collective-permute-start.8
  70.9 1.5 %collective-permute-start.7 = (f32[16,128]{1,0:T(8,128)S(1)}, f32[16,128]{1,0:T(8,128)S(1)}, u32[]{:S(2)}, u32[]{:S(2)}) collective-permute-start(f32[16,128]{1,0:T(8,128)S(1)} %shard_map.49), channel_id=1, source_target_pairs={{0,6},{2,4},{4,2},{6,0},{1,7},{3,5},{5,3},{7,1},{8,14},{10,12},{12... | collective-permute-start | bytes 24584 | tf_op jit(solution)/shard_map/ppermute | solution.py:31
  72.4 0.2 collective-permute-done.9
  72.6 1.1 collective-permute-done.8
  73.7 1.7 %collective-permute-done.7 = f32[16,128]{1,0:T(8,128)S(1)} collective-permute-done((f32[16,128]{1,0:T(8,128)S(1)}, f32[16,128]{1,0:T(8,128)S(1)}, u32[]{:S(2)}, u32[]{:S(2)}) %collective-permute-start.7) | collective-permute-done | bytes 8224 | tf_op jit(solution)/shard_map/ppermute | solution.py:31
  75.5 1.4 %collective-permute-start.12 = (f32[4,16,128]{2,1,0:T(8,128)S(1)}, f32[4,16,128]{2,1,0:T(8,128)S(1)}, u32[]{:S(2)}, u32[]{:S(2)}) collective-permute-start(f32[4,16,128]{2,1,0:T(8,128)S(1)} %pad_maximum_fusion.3), channel_id=1, source_target_pairs={{0,8},{8,0},{16,24},{24,16},{1,9},{9,1},{17,25},{25,17},{2,10},{10... | collective-permute-start | bytes 98312 | tf_op jit(solution)/shard_map/ppermute | solution.py:31
  76.9 0.0 collective-permute-start.11
  76.9 3.0 %collective-permute-start.10 = (f32[4,16,128]{2,1,0:T(8,128)S(1)}, f32[4,16,128]{2,1,0:T(8,128)S(1)}, u32[]{:S(2)}, u32[]{:S(2)}) collective-permute-start(f32[4,16,128]{2,1,0:T(8,128)S(1)} %pad_maximum_fusion.3), channel_id=1, source_target_pairs={{0,24},{8,16},{16,8},{24,0},{1,25},{9,17},{17,9},{25,1},{2,26},{10... | collective-permute-start | bytes 98312 | tf_op jit(solution)/shard_map/ppermute | solution.py:31
  79.9 0.0 collective-permute-done.12
  79.9 2.1 %collective-permute-done.11 = f32[4,16,128]{2,1,0:T(8,128)S(1)} collective-permute-done((f32[4,16,128]{2,1,0:T(8,128)S(1)}, f32[4,16,128]{2,1,0:T(8,128)S(1)}, u32[]{:S(2)}, u32[]{:S(2)}) %collective-permute-start.11) | collective-permute-done | bytes 32800 | tf_op jit(solution)/shard_map/ppermute | solution.py:31
  82.1 0.6 collective-permute-done.10
  82.7 0.4 shard_map.50.own_gram_ref
  83.1 0.1 collective-permute-start.13
  83.1 1.2 collective-permute-done.13.other_gram_ref
  84.3 0.0 all-to-all-done.block_ref
  84.3 1.5 %shard_map.51 = (f32[32,896]{1,0:T(8,128)S(1)}, f32[32,128]{1,0:T(8,128)}) custom-call(f32[32,32]{1,0:T(8,128)S(1)} %shard_map.50.own_gram_ref, f32[32,32]{1,0:T(8,128)S(1)} %collective-permute-done.13.other_gram_ref, f32[256,128]{1,0:T(8,128)S(1)} %bitcast.50, bf16[16,64,896]{2,1,0:T(8,128)(2,1)S(1)} %all-to-all-done.block_ref), custom_call_target="tpu_custom_call" | custom-call | flops 58720256 | bytes 1974272 | tf_op jit(solution)/shard_map/pallas_call | solution.py:44
  85.8 0.2 collective-permute-start.14
  86.1 1.2 collective-permute-done.14
  87.2 0.7 shard_map.52
  87.9 13.0 %all_to_all.20 = f32[16,16,128]{2,1,0:T(8,128)S(1)} all-to-all(f32[16,16,128]{2,1,0:T(8,128)S(1)} %shard_map.52), channel_id=1, replica_groups=mesh['rep'=1,'hi'=4,'lo'=4,'core'=2] {'hi','lo'}, dimensions={0} | all-to-all | bytes 262144 | tf_op jit(solution)/shard_map/all_to_all | solution.py:343
  100.9 10.7 %all_to_all.21 = f32[16,16,128]{2,1,0:T(8,128)S(1)} all-to-all(f32[16,16,128]{2,1,0:T(8,128)S(1)} %broadcast_in_dim.6), channel_id=1, replica_groups=mesh['rep'=1,'hi'=4,'lo'=4,'core'=2] {'hi','lo'}, dimensions={0} | all-to-all | bytes 262144 | tf_op jit(solution)/shard_map/all_to_all | solution.py:22
  111.7 0.4 shard_map.53.own_gram_ref
  112.0 0.1 collective-permute-start.15
  112.1 1.2 collective-permute-done.15.other_gram_ref
  113.3 1.5 %shard_map.54 = (f32[32,896]{1,0:T(8,128)S(1)}, f32[32,128]{1,0:T(8,128)S(1)}) custom-call(f32[32,32]{1,0:T(8,128)S(1)} %shard_map.53.own_gram_ref, f32[32,32]{1,0:T(8,128)S(1)} %collective-permute-done.15.other_gram_ref, f32[256,128]{1,0:T(8,128)S(1)} %bitcast.52, bf16[16,64,896]{2,1,0:T(8,128)(2,1)S(1)} %all-to-all-done.block_ref), custom_call_target="tpu_custom_call" | custom-call | flops 58720256 | bytes 1974272 | tf_op jit(solution)/shard_map/pallas_call | solution.py:44
  114.8 0.2 collective-permute-start.16
  115.0 1.2 collective-permute-done.16
  116.3 17.0 %all_to_all.22 = bf16[16,1,16,896]{3,2,1,0:T(8,128)(2,1)S(1)} all-to-all(bf16[16,1,16,896]{3,2,1,0:T(8,128)(2,1)S(1)} %broadcast_in_dim.7), channel_id=1, replica_groups=mesh['rep'=1,'hi'=4,'lo'=4,'core'=2] {'hi','lo'}, dimensions={0} | all-to-all | bytes 917504 | tf_op jit(solution)/shard_map/all_to_all | solution.py:22
  133.3 0.0 collective-permute-start.17
  133.3 1.0 shard_map.55
  134.3 1.5 %fetch.1.rows_ref = bf16[64,14336]{1,0:T(8,128)(2,1)S(1)} custom-call(bf16[64,14336]{1,0:T(8,128)(2,1)} %bitcast.45), custom_call_target="tpu_custom_call" | custom-call | flops 1000000 | bytes 3670016 | tf_op jit(solution)/shard_map/fetch/pallas_call | solution.py:249
  135.7 0.0 collective-permute-done.17.other_ref
  135.7 2.2 %residual.1 = (bf16[64,14336]{1,0:T(8,128)(2,1)}, f32[32,448]{1,0:T(8,128)}) custom-call(bf16[16,16,896]{2,1,0:T(8,128)(2,1)S(1)} %bitcast.48, bf16[16,16,896]{2,1,0:T(8,128)(2,1)S(1)} %collective-permute-done.17.other_ref, bf16[32,64]{1,0:T(8,128)(2,1)S(1)} %get-tuple-element.16.left_ref, f32[32,896]{1,0:T(8,128)S(1)} %add.14.q_ref, ...), custom_call_target="tpu_custom_call" | custom-call | flops 58720256 | bytes 3670016 | tf_op jit(solution)/shard_map/residual/pallas_call | solution.py:295
  (13 shorter events, 0.2 us)
Async XLA Ops:
  3.1 8.4 %copy-start.1 = (bf16[32,448]{1,0:T(8,128)(2,1)S(1)}, bf16[32,448]{1,0:T(8,128)(2,1)}, u32[]{:S(2)}) copy-start(bf16[32,448]{1,0:T(8,128)(2,1)} %param.3) | copy-start | bytes 86020
  3.1 81.2 %all-to-all-start = ((bf16[16,64,896]{2,1,0:T(8,128)(2,1)}), bf16[16,64,896]{2,1,0:T(8,128)(2,1)S(1)}, u32[]{:S(2)}, u32[]{:S(2)}) async-start(bf16[16,64,896]{2,1,0:T(8,128)(2,1)} %cut.1), calls=%async_computation | async-start | bytes 3670016 | tf_op jit(solution)/shard_map/all_to_all | solution.py:326
  11.6 31.0 %collective-permute-start.2 = (bf16[32,512]{1,0:T(8,128)(2,1)S(1)}, bf16[32,512]{1,0:T(8,128)(2,1)S(1)}, u32[]{:S(2)}, u32[]{:S(2)}) collective-permute-start(bf16[32,512]{1,0:T(8,128)(2,1)S(1)} %pad_select_fusion), channel_id=1, source_target_pairs={{0,8},{8,0},{16,24},{24,16},{1,9},{9,1},{17,25},{25,17},{2,10},{10... | collective-permute-start | bytes 98312 | tf_op jit(solution)/shard_map/ppermute | solution.py:31
  13.6 43.0 %collective-permute-start.1 = (bf16[32,512]{1,0:T(8,128)(2,1)S(1)}, bf16[32,512]{1,0:T(8,128)(2,1)S(1)}, u32[]{:S(2)}, u32[]{:S(2)}) collective-permute-start(bf16[32,512]{1,0:T(8,128)(2,1)S(1)} %pad_select_fusion), channel_id=1, source_target_pairs={{0,16},{8,24},{16,0},{24,8},{1,17},{9,25},{17,1},{25,9},{2,18},{10... | collective-permute-start | bytes 98312 | tf_op jit(solution)/shard_map/ppermute | solution.py:31
  15.9 40.6 %collective-permute-start = (bf16[32,512]{1,0:T(8,128)(2,1)S(1)}, bf16[32,512]{1,0:T(8,128)(2,1)S(1)}, u32[]{:S(2)}, u32[]{:S(2)}) collective-permute-start(bf16[32,512]{1,0:T(8,128)(2,1)S(1)} %pad_select_fusion), channel_id=1, source_target_pairs={{0,24},{8,16},{16,8},{24,0},{1,25},{9,17},{17,9},{25,1},{2,26},{10... | collective-permute-start | bytes 98312 | tf_op jit(solution)/shard_map/ppermute | solution.py:31
  56.7 6.4 %collective-permute-start.5 = (bf16[4,32,512]{2,1,0:T(8,128)(2,1)S(1)}, bf16[4,32,512]{2,1,0:T(8,128)(2,1)S(1)}, u32[]{:S(2)}, u32[]{:S(2)}) collective-permute-start(bf16[4,32,512]{2,1,0:T(8,128)(2,1)S(1)} %pad_maximum_fusion.1), channel_id=1, source_target_pairs={{0,2},{2,0},{4,6},{6,4},{1,3},{3,1},{5,7},{7,5},{8,10},{10,8},{12,... | collective-permute-start | bytes 393224 | tf_op jit(solution)/shard_map/ppermute | solution.py:31
  58.2 6.3 %collective-permute-start.4 = (bf16[4,32,512]{2,1,0:T(8,128)(2,1)S(1)}, bf16[4,32,512]{2,1,0:T(8,128)(2,1)S(1)}, u32[]{:S(2)}, u32[]{:S(2)}) collective-permute-start(bf16[4,32,512]{2,1,0:T(8,128)(2,1)S(1)} %pad_maximum_fusion.1), channel_id=1, source_target_pairs={{0,4},{2,6},{4,0},{6,2},{1,5},{3,7},{5,1},{7,3},{8,12},{10,14},{12... | collective-permute-start | bytes 393224 | tf_op jit(solution)/shard_map/ppermute | solution.py:31
  60.1 5.9 %collective-permute-start.3 = (bf16[4,32,512]{2,1,0:T(8,128)(2,1)S(1)}, bf16[4,32,512]{2,1,0:T(8,128)(2,1)S(1)}, u32[]{:S(2)}, u32[]{:S(2)}) collective-permute-start(bf16[4,32,512]{2,1,0:T(8,128)(2,1)S(1)} %pad_maximum_fusion.1), channel_id=1, source_target_pairs={{0,6},{2,4},{4,2},{6,0},{1,7},{3,5},{5,3},{7,1},{8,14},{10,12},{12... | collective-permute-start | bytes 393224 | tf_op jit(solution)/shard_map/ppermute | solution.py:31
  60.7 7.5 %copy-start = (bf16[1,64,14336]{2,1,0:T(8,128)(2,1)S(1)}, bf16[1,64,14336]{2,1,0:T(8,128)(2,1)}, u32[]{:S(2)}) copy-start(bf16[1,64,14336]{2,1,0:T(8,128)(2,1)} %param.2) | copy-start | bytes 5505028
  66.2 2.0 %collective-permute-start.6 = (bf16[4,4,32,512]{3,2,1,0:T(8,128)(2,1)S(1)}, bf16[4,4,32,512]{3,2,1,0:T(8,128)(2,1)S(1)}, u32[]{:S(2)}, u32[]{:S(2)}) collective-permute-start(bf16[4,4,32,512]{3,2,1,0:T(8,128)(2,1)S(1)} %pad_maximum_fusion.own_ref), channel_id=1, source_target_pairs={{0,1},{1,0},{2,3},{3,2},{4,5},{5,4},{6,7},{7,6},{8,9},{9,8},{10,11... | collective-permute-start | bytes 1572872 | tf_op jit(solution)/shard_map/ppermute | solution.py:17
  68.9 3.7 %collective-permute-start.9 = (f32[16,128]{1,0:T(8,128)S(1)}, f32[16,128]{1,0:T(8,128)S(1)}, u32[]{:S(2)}, u32[]{:S(2)}) collective-permute-start(f32[16,128]{1,0:T(8,128)S(1)} %shard_map.49), channel_id=1, source_target_pairs={{0,2},{2,0},{4,6},{6,4},{1,3},{3,1},{5,7},{7,5},{8,10},{10,8},{12,... | collective-permute-start | bytes 24584 | tf_op jit(solution)/shard_map/ppermute | solution.py:31
  70.1 3.7 %collective-permute-start.8 = (f32[16,128]{1,0:T(8,128)S(1)}, f32[16,128]{1,0:T(8,128)S(1)}, u32[]{:S(2)}, u32[]{:S(2)}) collective-permute-start(f32[16,128]{1,0:T(8,128)S(1)} %shard_map.49), channel_id=1, source_target_pairs={{0,4},{2,6},{4,0},{6,2},{1,5},{3,7},{5,1},{7,3},{8,12},{10,14},{12... | collective-permute-start | bytes 24584 | tf_op jit(solution)/shard_map/ppermute | solution.py:31
  70.9 4.5 %collective-permute-start.7 = (f32[16,128]{1,0:T(8,128)S(1)}, f32[16,128]{1,0:T(8,128)S(1)}, u32[]{:S(2)}, u32[]{:S(2)}) collective-permute-start(f32[16,128]{1,0:T(8,128)S(1)} %shard_map.49), channel_id=1, source_target_pairs={{0,6},{2,4},{4,2},{6,0},{1,7},{3,5},{5,3},{7,1},{8,14},{10,12},{12... | collective-permute-start | bytes 24584 | tf_op jit(solution)/shard_map/ppermute | solution.py:31
  75.5 4.5 %collective-permute-start.12 = (f32[4,16,128]{2,1,0:T(8,128)S(1)}, f32[4,16,128]{2,1,0:T(8,128)S(1)}, u32[]{:S(2)}, u32[]{:S(2)}) collective-permute-start(f32[4,16,128]{2,1,0:T(8,128)S(1)} %pad_maximum_fusion.3), channel_id=1, source_target_pairs={{0,8},{8,0},{16,24},{24,16},{1,9},{9,1},{17,25},{25,17},{2,10},{10... | collective-permute-start | bytes 98312 | tf_op jit(solution)/shard_map/ppermute | solution.py:31
  76.9 5.2 %collective-permute-start.11 = (f32[4,16,128]{2,1,0:T(8,128)S(1)}, f32[4,16,128]{2,1,0:T(8,128)S(1)}, u32[]{:S(2)}, u32[]{:S(2)}) collective-permute-start(f32[4,16,128]{2,1,0:T(8,128)S(1)} %pad_maximum_fusion.3), channel_id=1, source_target_pairs={{0,16},{8,24},{16,0},{24,8},{1,17},{9,25},{17,1},{25,9},{2,18},{10... | collective-permute-start | bytes 98312 | tf_op jit(solution)/shard_map/ppermute | solution.py:31
  76.9 5.7 %collective-permute-start.10 = (f32[4,16,128]{2,1,0:T(8,128)S(1)}, f32[4,16,128]{2,1,0:T(8,128)S(1)}, u32[]{:S(2)}, u32[]{:S(2)}) collective-permute-start(f32[4,16,128]{2,1,0:T(8,128)S(1)} %pad_maximum_fusion.3), channel_id=1, source_target_pairs={{0,24},{8,16},{16,8},{24,0},{1,25},{9,17},{17,9},{25,1},{2,26},{10... | collective-permute-start | bytes 98312 | tf_op jit(solution)/shard_map/ppermute | solution.py:31
  83.1 1.2 collective-permute-start.13
  85.8 1.4 %collective-permute-start.14 = (f32[32,896]{1,0:T(8,128)S(1)}, f32[32,896]{1,0:T(8,128)S(1)}, u32[]{:S(2)}, u32[]{:S(2)}) collective-permute-start(f32[32,896]{1,0:T(8,128)S(1)} %get-tuple-element.12), channel_id=1, source_target_pairs={{0,1},{1,0},{2,3},{3,2},{4,5},{5,4},{6,7},{7,6},{8,9},{9,8},{10,11... | collective-permute-start | bytes 344072 | tf_op jit(solution)/shard_map/ppermute | solution.py:17
  112.0 1.2 collective-permute-start.15
  114.8 1.4 %collective-permute-start.16 = (f32[32,896]{1,0:T(8,128)S(1)}, f32[32,896]{1,0:T(8,128)S(1)}, u32[]{:S(2)}, u32[]{:S(2)}) collective-permute-start(f32[32,896]{1,0:T(8,128)S(1)} %get-tuple-element.13), channel_id=1, source_target_pairs={{0,1},{1,0},{2,3},{3,2},{4,5},{5,4},{6,7},{7,6},{8,9},{9,8},{10,11... | collective-permute-start | bytes 344072 | tf_op jit(solution)/shard_map/ppermute | solution.py:17
  133.3 2.5 %collective-permute-start.17 = (bf16[16,16,896]{2,1,0:T(8,128)(2,1)S(1)}, bf16[16,16,896]{2,1,0:T(8,128)(2,1)S(1)}, u32[]{:S(2)}, u32[]{:S(2)}) collective-permute-start(bf16[16,16,896]{2,1,0:T(8,128)(2,1)S(1)} %bitcast.47), channel_id=1, source_target_pairs={{0,1},{1,0},{2,3},{3,2},{4,5},{5,4},{6,7},{7,6},{8,9},{9,8},{10,11... | collective-permute-start | bytes 1376264 | tf_op jit(solution)/shard_map/ppermute | solution.py:17
